TPU v7x, 32 devices: a whole 2x2x4 slice. The times are simulated.
32 devices in a mesh: grp: 2 (over y), row: 16 (over z, x, core).
Axes of the slice: x: 2, y: 2, z: 4, core: 2. Of those that a mesh axis runs over, the one named last changes fastest.
Arguments:
- queries: bfloat16 [4096, 4096], P(('grp', 'row')), parts along dimension 0, may hold values from -130 to 130
- answer_keys: bfloat16 [4096, 512], P(('grp', 'row')), parts along dimension 0, may hold values from -6 to 6
- answer_values: bfloat16 [4096, 512], P(('grp', 'row')), parts along dimension 0, may hold values from -6 to 6
- prompt_keys: bfloat16 [256, 512], P(('grp', 'row')), parts along dimension 0, may hold values from -4 to 4
- prompt_values: bfloat16 [256, 512], P(('grp', 'row')), parts along dimension 0, may hold values from -6 to 6
- out_grad: bfloat16 [4096, 4096], P(('grp', 'row')), parts along dimension 0, may hold values from -6 to 6
- weights: float32 [4096], P(('grp', 'row')), parts along dimension 0, may hold values from 0.25 to 4
- lengths: int32 [64], P('grp'), parts along dimension 0, may hold values from 1 to 256, as said below
Outputs:
- attn_out: bfloat16 [4096, 4096], P(('grp', 'row')), parts along dimension 0
- q_grad: bfloat16 [4096, 4096], P(('grp', 'row')), parts along dimension 0
- answer_key_grad: bfloat16 [4096, 512], P(('grp', 'row')), parts along dimension 0
- answer_value_grad: bfloat16 [4096, 512], P(('grp', 'row')), parts along dimension 0
- prompt_key_grad: float32 [256, 512], P(('grp', 'row')), parts along dimension 0
- prompt_value_grad: float32 [256, 512], P(('grp', 'row')), parts along dimension 0
There are 2 independent parts, one for each index of `grp`. A program takes and returns all parts, laid end to end along the dimension named above; each array names one. Nothing has to cross between parts.
Inputs may be any that keep to these rules, and one draw needn't show every extreme that they name: `lengths`: the answers fill the 2048 packed rows in order; the longest has exactly 256 rows.
All inputs are finite; a program needn't handle non-finite values.
Results may differ from a plain program's by a relative error of at most 0.02.
Values may be sent and summed in bfloat16 or wider, within the bound.
A program may use at most 192 MiB of HBM per device.

v0:
```python
import functools
import math

import jax
import jax.numpy as jnp
from jax import lax
from jax.experimental import pallas as pl
from jax.experimental.pallas import tpu as pltpu
from jax.sharding import PartitionSpec as P

HEAD_DIM = 128
MASKED = -1e30
MESH = pl.DeviceIdType.MESH


def dot(a, b):
    return jnp.dot(a, b, preferred_element_type=jnp.float32)


def twice(x):
    return jnp.concatenate([x, x], axis=1)


def kernel(
    n, kv_heads, group,
    q_hbm, og_hbm, ak, av, pk, pv, w, lens,
    attn_v, dq_v, akg, avg, pkg, pvg,
    ogv, win, pst, pgath, psend, pmid, pred, precv,
    gsend, gmid, gout, grecv, own,
    qs, qs_t, cots, cots_t, kcat, vcat, kt, vt, p_all, ds_all, bias, tri_b, wfull,
    in_sem, st_sem, win_send, win_recv, wr_send, pg_send, pg_recv, pp_send, pp_recv,
    pm_send, pm_recv, pr_send, pr_recv, gm_send, gm_recv, gr_send, gr_recv,
):
    me = lax.axis_index("row")
    height = ak.shape[0]
    d = HEAD_DIM
    span = group * d
    prompt = pk.shape[0] * n
    factor = d ** (-0.5)
    log_factor = factor * math.log2(math.e)

    chips = n // 2
    core = lax.rem(me, 2)
    chip = me // 2
    sibling = me + 1 - 2 * core
    across = lax.rem(me + n - 1 + 2 * core, n)

    def same(k):
        return lax.rem(me + 2 * k, n)

    def remote(src, dst, send, recv, target):
        return pltpu.make_async_remote_copy(
            src_ref=src, dst_ref=dst, send_sem=send, recv_sem=recv,
            device_id={"row": target}, device_id_type=MESH,
        )

    def cols(g, width):
        return pl.ds(pl.multiple_of(g * width, width), width)

    def q_copy(g, h):
        return pltpu.make_async_copy(
            q_hbm.at[:, pl.ds((g * group + h) * d, d)],
            qs.at[g, pl.ds(h * height, height)], in_sem.at[g, 0],
        )

    def og_copy(g):
        return pltpu.make_async_copy(og_hbm.at[:, cols(g, span)], ogv.at[g], in_sem.at[g, 1])

    def stage_copies(g):
        return (
            pltpu.make_async_copy(pk.at[:, cols(g, d)], pst.at[g, 0], st_sem.at[g, 0]),
            pltpu.make_async_copy(pv.at[:, cols(g, d)], pst.at[g, 1], st_sem.at[g, 1]),
        )

    def win_copy(g, far, which):
        return remote(
            (ak, av)[which].at[:, cols(g, d)], win.at[g, far, which],
            win_send.at[g, far, which], win_recv.at[g, far, which],
            same(1) if far else lax.rem(me + 1, n),
        )

    def win_relay(g, which):
        return remote(
            win.at[g, 0, which], win.at[g, 1, which],
            wr_send.at[g, which], win_recv.at[g, 1, which], sibling,
        )

    def gather_copy(g, k):
        return remote(
            pst.at[g], pgath.at[g, core, chip], pg_send.at[g], pg_recv.at[g], same(k)
        )

    def gather_relay(g):
        return remote(
            pgath.at[g, core], pgath.at[g, core], pp_send.at[g], pp_recv.at[g], sibling
        )

    def pair_copy(g):
        return remote(psend.at[g, 1 - core], pmid.at[g], pm_send.at[g], pm_recv.at[g], sibling)

    def reduce_copy(g, k):
        return remote(
            pred.at[g, lax.rem(chip + k, chips)], precv.at[g, chip],
            pr_send.at[g], pr_recv.at[g], same(k),
        )

    def mid_copy(g):
        return remote(gsend.at[g], gmid.at[g], gm_send.at[g], gm_recv.at[g], sibling)

    def back_copy(g, far):
        return remote(
            gsend.at[g, 1] if far else gout.at[g], grecv.at[g],
            gr_send.at[g, far], gr_recv.at[g], same(chips - 1) if far else across,
        )

    def relay(g):
        for which in range(2):
            win_copy(g, 0, which).wait_recv()

        @pl.when(core == 0)
        def _():
            for which in range(2):
                win_relay(g, which).start()

        here = pgath.at[g, core]
        pltpu.make_async_copy(here, here, pg_recv.at[g]).wait()
        gather_relay(g).start()

    def pass_on(g):
        pair_copy(g).wait_recv()
        pred[g] = (psend[g, core] + pmid[g]).astype(jnp.bfloat16)

        @pl.when(core == 0)
        def _():
            mid_copy(g).wait_recv()
            gout[g] = (
                gsend[g, 0].astype(jnp.float32) + gmid[g, 1].astype(jnp.float32)
            ).astype(jnp.bfloat16)
            own[g] = own[g] + gmid[g, 0].astype(jnp.float32)
            back_copy(g, 0).start()
            back_copy(g, 1).start()

        pltpu.make_async_copy(pred.at[g, chip], precv.at[g, chip], pr_recv.at[g]).start()

        @pl.loop(1, chips)
        def _(k):
            reduce_copy(g, k).start()

    barrier = pltpu.get_barrier_semaphore()

    @pl.loop(1, chips)
    def _(k):
        pl.semaphore_signal(barrier, inc=1, device_id={"row": same(k)}, device_id_type=MESH)

    for target in (sibling, across):
        pl.semaphore_signal(barrier, inc=1, device_id={"row": target}, device_id_type=MESH)

    for g in range(kv_heads):
        for copy in stage_copies(g):
            copy.start()
    for g in range(kv_heads):
        og_copy(g).start()
    for g in range(kv_heads):
        for h in range(group):
            q_copy(g, h).start()

    answers = lens.shape[1]
    row = lax.broadcasted_iota(jnp.int32, (answers, answers), 0)
    col = lax.broadcasted_iota(jnp.int32, (answers, answers), 1)
    starts = jnp.sum(
        jnp.where(col < row, jnp.broadcast_to(lens[...], (answers, answers)), 0),
        axis=1, keepdims=True,
    )
    pos = me * height + lax.broadcasted_iota(jnp.int32, (1, height), 1)
    first = jnp.max(jnp.where(starts <= pos, starts, 0), axis=0, keepdims=True)
    key = lax.broadcasted_iota(jnp.int32, (height, height), 0)
    query = lax.broadcasted_iota(jnp.int32, (height, height), 1)
    tri = key <= query
    base = me * height
    near = jnp.where(key + (base - height) >= first, 0.0, MASKED)
    both = jnp.where(tri, key + base, key + (base - 2 * height))
    both = jnp.where(both >= first, 0.0, MASKED)
    bias[0] = near
    bias[1] = both
    tri_b[...] = tri.astype(jnp.float32).astype(jnp.bfloat16)
    wfull[...] = jnp.broadcast_to(w[...], (height, height)).T

    def prepare(g):
        og_copy(g).wait()
        for h in range(group):
            rows = slice(h * height, (h + 1) * height)
            cot = wfull[...] * ogv[g, :, h * d : (h + 1) * d].astype(jnp.float32)
            cot = cot.astype(jnp.bfloat16)
            cots[g, rows, :] = cot
            cots_t[g, :, rows] = cot.T

    @pl.loop(0, kv_heads)
    def _(g):
        prepare(g)

    for g in range(kv_heads):
        for copy in stage_copies(g):
            copy.wait()
    pl.semaphore_wait(barrier, chips + 1)

    @pl.loop(0, kv_heads)
    def _(g):
        pltpu.make_async_copy(pst.at[g], pgath.at[g, core, chip], pg_recv.at[g]).start()

        @pl.loop(1, chips)
        def _(k):
            gather_copy(g, k).start()

        for which in range(2):
            win_copy(g, 0, which).start()

        @pl.when(core == 0)
        def _():
            for which in range(2):
                win_copy(g, 1, which).start()

    @pl.loop(0, kv_heads)
    def _(g):
        mine = qs.at[g]
        pltpu.make_async_copy(mine, mine, in_sem.at[g, 0]).wait()
        for h in range(group):
            rows = slice(h * height, (h + 1) * height)
            qs_t[g, :, rows] = qs[g, rows, :].T

    relay(0)

    @pl.loop(0, kv_heads)
    def _(g):
        there = pgath.at[g, 1 - core]
        pltpu.make_async_copy(there, there, pp_recv.at[g]).wait()
        for which in range(2):
            win_copy(g, 1, which).wait_recv()
        at1, at2, at3 = prompt, prompt + height, prompt + 2 * height
        for which, (cat, tr, mine) in enumerate(((kcat, kt, ak), (vcat, vt, av))):
            gathered = pgath[g, :, :, which].astype(jnp.float32).reshape(prompt, d)
            cat[:at1, :] = gathered.astype(jnp.bfloat16)
            cat[at1:at2, :] = win[g, 0, which]
            cat[at2:at3, :] = win[g, 1, which]
            cat[at3:, :] = mine[:, cols(g, d)]
            tr[...] = cat[...].T
        tri2 = twice(tri)
        for pair in range(group // 2):
            rows = slice(pair * 2 * height, (pair + 1) * 2 * height)
            s = dot(kcat[...], qs_t[g, :, rows])
            s_p = s[:at1]
            s_1 = s[at1:at2] + twice(bias[0])
            s_c = jnp.where(tri2, s[at3:], s[at2:at3]) + twice(bias[1])
            top = jnp.maximum(
                jnp.maximum(jnp.max(s_p, axis=0, keepdims=True), jnp.max(s_1, axis=0, keepdims=True)),
                jnp.max(s_c, axis=0, keepdims=True),
            )
            e_p = jnp.exp2((s_p - top) * log_factor)
            e_1 = jnp.exp2((s_1 - top) * log_factor)
            e_c = jnp.exp2((s_c - top) * log_factor)
            total = (
                jnp.sum(e_p, axis=0, keepdims=True)
                + jnp.sum(e_1, axis=0, keepdims=True)
                + jnp.sum(e_c, axis=0, keepdims=True)
            )
            inv = 1.0 / total
            c_p, c_1, c_c = e_p * inv, e_1 * inv, e_c * inv
            trib2 = twice(tri_b[...])
            p_all[:at1, rows] = c_p.astype(jnp.bfloat16)
            p_all[at1:at2, rows] = c_1.astype(jnp.bfloat16)
            b_c = c_c.astype(jnp.bfloat16)
            b_d = b_c * trib2
            p_all[at2:at3, rows] = b_c - b_d
            p_all[at3:, rows] = b_d
            out_t = dot(vt[...], p_all[:, rows]).astype(jnp.bfloat16)
            cot_t = cots_t[g, :, rows]
            delta = jnp.sum(
                cot_t.astype(jnp.float32) * out_t.astype(jnp.float32), axis=0, keepdims=True
            )
            slopes = dot(vcat[...], cot_t)
            ds_all[:at1, rows] = (c_p * (slopes[:at1] - delta)).astype(jnp.bfloat16)
            ds_all[at1:at2, rows] = (c_1 * (slopes[at1:at2] - delta)).astype(jnp.bfloat16)
            s_c = jnp.where(tri2, slopes[at3:], slopes[at2:at3])
            g_c = (c_c * (s_c - delta)).astype(jnp.bfloat16)
            g_d = g_c * trib2
            ds_all[at2:at3, rows] = g_c - g_d
            ds_all[at3:, rows] = g_d
            out = out_t.T
            for j in range(2):
                lanes = slice((2 * pair + j) * d, (2 * pair + j + 1) * d)
                attn_v[g, :, lanes] = out[j * height : (j + 1) * height]
        for which in range(2):
            if which == 0:
                part = dot(ds_all[...], qs[g]) * factor
            else:
                part = dot(p_all[...], cots[g])
            psend[g, :, :, which] = part[:at1].reshape(2, chips, prompt // n, d)
            gsend[g, 0, which] = part[at1:at2].astype(jnp.bfloat16)
            gsend[g, 1, which] = part[at2:at3].astype(jnp.bfloat16)
            own[g, which] = part[at3:]
        pair_copy(g).start()

        @pl.when(core == 1)
        def _():
            mid_copy(g).start()

        @pl.when(g < kv_heads - 1)
        def _():
            relay(g + 1)

        dq_t = (dot(kt[...], ds_all[...]) * factor).astype(jnp.bfloat16)
        for h in range(group):
            rows = slice(h * height, (h + 1) * height)
            dq_v[g, :, h * d : (h + 1) * d] = dq_t[:, rows].T
        pass_on(g)

    for g in range(kv_heads):
        lanes = slice(g * d, (g + 1) * d)
        back_copy(g, 0).wait_recv()
        for which, grad in enumerate((akg, avg)):
            grad[:, lanes] = (own[g, which] + grecv[g, which].astype(jnp.float32)).astype(
                jnp.bfloat16
            )
        pltpu.make_async_copy(precv.at[g], precv.at[g], pr_recv.at[g]).wait()
        for which, grad in enumerate((pkg, pvg)):
            grad[:, lanes] = jnp.sum(precv[g, :, which].astype(jnp.float32), axis=0)

    for g in range(kv_heads):
        pair_copy(g).wait_send()
        gather_relay(g).wait_send()
        for which in range(2):
            win_copy(g, 0, which).wait_send()
        sent = pgath.at[g, 0, pl.ds(0, chips - 1)]
        pltpu.make_async_copy(sent, sent, pg_send.at[g]).wait()
        sent = precv.at[g, pl.ds(0, chips - 1)]
        pltpu.make_async_copy(sent, sent, pr_send.at[g]).wait()

        @pl.when(core == 0)
        def _():
            for which in range(2):
                win_copy(g, 1, which).wait_send()
                win_relay(g, which).wait_send()
                back_copy(g, which).wait_send()

        @pl.when(core == 1)
        def _():
            mid_copy(g).wait_send()


def write_out(kv_heads, span, attn_v, dq_v, akg, avg, pkg, pvg, *refs):
    outs, (wide_sem, sem) = refs[:6], refs[6:]
    copies = [
        pltpu.make_async_copy(v.at[g], out.at[:, pl.ds(g * span, span)], wide_sem.at[i, g])
        for i, (v, out) in enumerate(((attn_v, outs[0]), (dq_v, outs[1])))
        for g in range(kv_heads)
    ] + [
        pltpu.make_async_copy(v, out, sem.at[i])
        for i, (v, out) in enumerate(zip((akg, avg, pkg, pvg), outs[2:]))
    ]
    for copy in copies:
        copy.start()
    for copy in copies:
        copy.wait()


def per_device(n, queries, answer_keys, answer_values, prompt_keys, prompt_values, out_grad, weights, lengths):
    height = queries.shape[0]
    d = HEAD_DIM
    columns = answer_keys.shape[1]
    kv_heads = columns // d
    group = queries.shape[1] // columns
    own_prompt = prompt_keys.shape[0]
    keys = own_prompt * n + 3 * height
    span = group * d
    bf16, f32 = jnp.bfloat16, jnp.float32
    vmem = pl.BlockSpec(memory_space=pltpu.VMEM)
    hbm = pl.BlockSpec(memory_space=pltpu.HBM)
    dma = pltpu.SemaphoreType.DMA
    results = pl.pallas_call(
        functools.partial(kernel, n, kv_heads, group),
        out_shape=(
            pltpu.VMEM((kv_heads, height, span), bf16),
            pltpu.VMEM((kv_heads, height, span), bf16),
            pltpu.VMEM(answer_keys.shape, bf16),
            pltpu.VMEM(answer_keys.shape, bf16),
            pltpu.VMEM(prompt_keys.shape, f32),
            pltpu.VMEM(prompt_keys.shape, f32),
        ),
        in_specs=[hbm, hbm] + [vmem] * 6,
        out_specs=(vmem,) * 6,
        scratch_shapes=[
            pltpu.VMEM((kv_heads, height, span), bf16),
            pltpu.VMEM((kv_heads, 2, 2, height, d), bf16),
            pltpu.VMEM((kv_heads, 2, own_prompt, d), bf16),
            pltpu.VMEM((kv_heads, 2, n // 2, 2, own_prompt, d), bf16),
            pltpu.VMEM((kv_heads, 2, n // 2, 2, own_prompt, d), f32),
            pltpu.VMEM((kv_heads, n // 2, 2, own_prompt, d), f32),
            pltpu.VMEM((kv_heads, n // 2, 2, own_prompt, d), bf16),
            pltpu.VMEM((kv_heads, n // 2, 2, own_prompt, d), bf16),
            pltpu.VMEM((kv_heads, 2, 2, height, d), bf16),
            pltpu.VMEM((kv_heads, 2, 2, height, d), bf16),
            pltpu.VMEM((kv_heads, 2, height, d), bf16),
            pltpu.VMEM((kv_heads, 2, height, d), bf16),
            pltpu.VMEM((kv_heads, 2, height, d), f32),
            pltpu.VMEM((kv_heads, group * height, d), bf16),
            pltpu.VMEM((kv_heads, d, group * height), bf16),
            pltpu.VMEM((kv_heads, group * height, d), bf16),
            pltpu.VMEM((kv_heads, d, group * height), bf16),
            pltpu.VMEM((keys, d), bf16),
            pltpu.VMEM((keys, d), bf16),
            pltpu.VMEM((d, keys), bf16),
            pltpu.VMEM((d, keys), bf16),
            pltpu.VMEM((keys, group * height), bf16),
            pltpu.VMEM((keys, group * height), bf16),
            pltpu.VMEM((2, height, height), f32),
            pltpu.VMEM((height, height), bf16),
            pltpu.VMEM((height, height), f32),
            dma((kv_heads, 2)),
            dma((kv_heads, 2)),
            dma((kv_heads, 2, 2)),
            dma((kv_heads, 2, 2)),
            dma((kv_heads, 2)),
            *[dma((kv_heads,))] * 10,
            dma((kv_heads, 2)),
            dma((kv_heads,)),
        ],
        compiler_params=pltpu.CompilerParams(
            collective_id=0, has_side_effects=True, vmem_limit_bytes=60 * 1024 * 1024
        ),
    )(
        queries, out_grad, answer_keys, answer_values, prompt_keys, prompt_values,
        weights.reshape(1, height), lengths.reshape(1, lengths.shape[0]),
    )
    return pl.pallas_call(
        functools.partial(write_out, kv_heads, span),
        out_shape=(
            jax.ShapeDtypeStruct(queries.shape, bf16),
            jax.ShapeDtypeStruct(queries.shape, bf16),
            jax.ShapeDtypeStruct(answer_keys.shape, bf16),
            jax.ShapeDtypeStruct(answer_keys.shape, bf16),
            jax.ShapeDtypeStruct(prompt_keys.shape, f32),
            jax.ShapeDtypeStruct(prompt_keys.shape, f32),
        ),
        in_specs=[vmem] * 6,
        out_specs=(hbm,) * 6,
        scratch_shapes=[dma((2, kv_heads)), dma((4,))],
        compiler_params=pltpu.CompilerParams(vmem_limit_bytes=4 * 1024 * 1024),
    )(*results)


def solution(mesh):
    both = ("grp", "row")
    wide = P(both, None)
    return jax.shard_map(
        functools.partial(per_device, mesh.shape["row"]),
        mesh=mesh,
        in_specs=(wide,) * 6 + (P(both), P("grp")),
        out_specs=(wide,) * 6,
        check_vma=False,
    )
```

profile of v0, /device:TPU:0, one launch (start us, length us, event | category | flops | bytes accessed | tf_op | source)
XLA Modules:
  0.0 34.0 jit_solution(16943729022715733196)
XLA Ops:
  0.6 31.9 %shard_map.127 = (bf16[4,128,1024]{2,1,0:T(8,128)(2,1)S(1)}, bf16[4,128,1024]{2,1,0:T(8,128)(2,1)S(1)}, bf16[128,512]{1,0:T(8,128)(2,1)S(1)}, bf16[128,512]{1,0:...) custom-call(bf16[128,4096]{1,0:T(8,128)(2,1)} %q_hbm.1, bf16[128,4096]{1,0:T(8,128)(2,1)} %og_hbm.1, ...), custom_call_target="tpu_custom_call" | custom-call | tf_op jit(solution)/shard_map/pallas_call | solution.py:378
  32.5 1.5 %shard_map.128 = (bf16[128,4096]{1,0:T(8,128)(2,1)}, bf16[128,4096]{1,0:T(8,128)(2,1)}, bf16[128,512]{1,0:T(8,128)(2,1)}, bf16[128,512]{1,0:T(8,128)(2,1)}, f32[8,512]{1,0:T(8,128)}, /*index=5*/f32[8,512]{1,0:T(8,128)}) custom-call(bf16[4,128,1024]{2,1,0:T(8,128)(2,1)S(1)} %get-tuple-element.12.attn_v, bf16[4,128,1024]{2,1,0:T(8,128)(2,1)S(1)} %get-tuple-element.13.dq_v, ...), custom_call_target="tpu_custom_call" | custom-call | tf_op jit(solution)/shard_map/pallas_call | solution.py:433
where the time goes:
time: 34.2 us; the launch traced here: 34 us
  Pallas kernels  33.4 us (98%)
  between operations  0.64 us (2%)
    pallas_call x1, Pallas kernels, per_device(): pl.pallas_call(functools.partial(kernel, n, kv_heads, group), out_shape=(...  31.9 us
    pallas_call x1, Pallas kernels, per_device(): pl.pallas_call(functools.partial(write_out, kv_heads, span), out_shape=(j...  1.51 us

commit v1 on v0

v1 whole, which is shorter than its diff:
```python
import functools
import math

import jax
import jax.numpy as jnp
from jax import lax
from jax.experimental import pallas as pl
from jax.experimental.pallas import tpu as pltpu
from jax.sharding import PartitionSpec as P

HEAD_DIM = 128
MASKED = -1e30
MESH = pl.DeviceIdType.MESH


def dot(a, b):
    return jnp.dot(a, b, preferred_element_type=jnp.float32)


def twice(x):
    return jnp.concatenate([x, x], axis=1)


def kernel(
    n, kv_heads, group,
    q_hbm, og_hbm, ak, av, pk, pv, w, lens,
    attn, dq, akg, avg, pkg, pvg,
    qog, kall, vt, kt, pgath, wst, lst, qs_t, cots, cots_t, p_all, ds_all, acc,
    psend, precv, gsend, grecv, srecv, bias, tri_b,
    small_sem, in_sem, kv_sem, xq_recv, xk_recv, win_recv, pg_recv, pr_recv, gr_recv, sr_recv, at_recv, dq_recv,
    xs_send, xq_send, xk_send, win_send, pg_send, pr_send, gs_send, sr_send, at_send, dq_send, w_recv, w_send,
):
    me = lax.axis_index("row")
    height = ak.shape[0]
    d = HEAD_DIM
    span = group * d
    half = kv_heads // 2
    own_prompt = pk.shape[0]
    prompt = own_prompt * n
    factor = d ** (-0.5)
    log_factor = factor * math.log2(math.e)
    chips = n // 2
    core = lax.rem(me, 2)
    other = 1 - core
    chip = me // 2
    sibling = me + 1 - 2 * core
    after = lax.rem(chip + 1, chips)
    before = lax.rem(chip + chips - 1, chips)
    at1, at2, at3 = prompt, prompt + height, prompt + 2 * height

    def remote(src, dst, send, recv, target):
        return pltpu.make_async_remote_copy(
            src_ref=src, dst_ref=dst, send_sem=send, recv_sem=recv,
            device_id={"row": target}, device_id_type=MESH,
        )

    def cols(at, width):
        return pl.ds(pl.multiple_of(at * width, width), width)

    def block(b):
        return pl.ds(pl.multiple_of(prompt + b * height, height), height)

    def in_copies(j):
        head = core * half + j
        return (
            pltpu.make_async_copy(q_hbm.at[:, cols(head, span)], qog.at[1, j, 0], in_sem.at[j]),
            pltpu.make_async_copy(og_hbm.at[:, cols(head, span)], qog.at[1, j, 1], in_sem.at[j]),
        )

    def cross_copies(j):
        head = other * half + j
        return (
            remote(og_hbm.at[:, cols(head, span)], qog.at[0, j, 1], xq_send.at[j], xq_recv.at[j], sibling),
            remote(q_hbm.at[:, cols(head, span)], qog.at[0, j, 0], xq_send.at[j], xq_recv.at[j], sibling),
        )

    def kv_copies(j):
        head = core * half + j
        return [
            pltpu.make_async_copy(src.at[:, cols(head, d)], kall.at[j, i, block(2 + core)], kv_sem.at[j])
            for i, src in enumerate((ak, av))
        ]

    def kv_cross(j):
        head = other * half + j
        return [
            remote(src.at[:, cols(head, d)], kall.at[j, i, block(2 + core)], xk_send.at[j], xk_recv.at[j], sibling)
            for i, src in enumerate((ak, av))
        ]

    def win_copies(j):
        return [
            remote(
                src.at[:, pl.ds((t * half + j) * d, d)], kall.at[j, i, block(core)],
                win_send.at[j], win_recv.at[j], 2 * after + t,
            )
            for i, src in enumerate((ak, av)) for t in range(2)
        ]

    def prompt_copy(k, i):
        target = lax.rem(me + k, n)
        return remote(
            (pk, pv)[i].at[:, cols(lax.rem(target, 2), half * d)], pgath.at[i, me],
            pg_send, pg_recv, target,
        )

    def reduce_copy(j, k):
        target = lax.rem(me + k, n)
        return remote(psend.at[j, target], precv.at[core, j, chip], pr_send.at[j], pr_recv.at[j], target)

    def back_copy(j, t):
        return remote(gsend.at[j, t], grecv.at[core, j], gs_send.at[j], gr_recv.at[j], 2 * before + t)

    def sibling_copy(j):
        return remote(acc.at[j, :, block(2 + other)], srecv.at[j], sr_send.at[j], sr_recv.at[j], sibling)

    def out_copy(ref, j, send, recv):
        return remote(ref.at[0, j], ref.at[2, j], send.at[j], recv.at[j], sibling)

    barrier = pltpu.get_barrier_semaphore()

    @pl.loop(1, n)
    def _(k):
        pl.semaphore_signal(barrier, inc=1, device_id={"row": lax.rem(me + k, n)}, device_id_type=MESH)

    w_local = pltpu.make_async_copy(w, wst.at[1], small_sem.at[0])
    lens_local = pltpu.make_async_copy(lens, lst, small_sem.at[1])
    own_prompts = [
        pltpu.make_async_copy((pk, pv)[i].at[:, cols(core, half * d)], pgath.at[i, me], pg_recv) for i in range(2)
    ]
    w_local.start()
    lens_local.start()
    for j in range(half):
        for copy in in_copies(j):
            copy.start()
    for j in range(half):
        for copy in kv_copies(j):
            copy.start()
    for copy in own_prompts:
        copy.start()
    pl.semaphore_wait(barrier, n - 1)

    @pl.loop(1, n)
    def _(k):
        for i in range(2):
            prompt_copy(k, i).start()

    w_cross = remote(w, wst.at[0], w_send, w_recv, sibling)
    w_cross.start()
    for j in range(half):
        for copy in win_copies(j):
            copy.start()
        for copy in cross_copies(j):
            copy.start()
        for copy in kv_cross(j):
            copy.start()

    acc[...] = jnp.zeros(acc.shape, jnp.float32)
    lens_local.wait()
    answers = lens.shape[1]
    row = lax.broadcasted_iota(jnp.int32, (answers, answers), 0)
    col = lax.broadcasted_iota(jnp.int32, (answers, answers), 1)
    starts = jnp.sum(
        jnp.where(col < row, jnp.broadcast_to(lst[...], (answers, answers)), 0),
        axis=1, keepdims=True,
    )
    key = lax.broadcasted_iota(jnp.int32, (height, height), 0)
    query = lax.broadcasted_iota(jnp.int32, (height, height), 1)
    tri = key <= query
    for b in range(2):
        base = (2 * chip + b) * height
        pos = base + lax.broadcasted_iota(jnp.int32, (1, height), 1)
        first = jnp.max(jnp.where(starts <= pos, starts, 0), axis=0, keepdims=True)
        bias[b, 0] = jnp.where(key + (base - height) >= first, 0.0, MASKED)
        both = jnp.where(tri, key + base, key + (base - 2 * height))
        bias[b, 1] = jnp.where(both >= first, 0.0, MASKED)
    tri_b[...] = tri.astype(jnp.float32).astype(jnp.bfloat16)

    def prepare(s, j):
        for h in range(group):
            rows = slice(h * height, (h + 1) * height)
            og_t = qog[s, j, 1, :, rows].T
            cots_t[s, j, :, rows] = (wst[s] * og_t.astype(jnp.float32)).astype(jnp.bfloat16)
            qs_t[s, j, :, rows] = qog[s, j, 0, :, rows].T

    w_local.wait()

    @pl.loop(0, half)
    def _(j):
        pltpu.make_async_copy(qog.at[1, j], qog.at[1, j], in_sem.at[j]).wait()
        prepare(1, j)

    w_cross.wait_recv()

    @pl.loop(0, half)
    def _(j):
        pltpu.make_async_copy(qog.at[0, j], qog.at[0, j], xq_recv.at[j]).wait()
        prepare(0, j)

    pltpu.make_async_copy(pgath, pgath, pg_recv).wait()

    @pl.loop(0, 2 * half)
    def _(u):
        j = u // 2
        s = lax.rem(u, 2)
        b = s * core + (1 - s) * other

        @pl.when(s == 0)
        def _():
            mine = kall.at[j, :, block(2 + core)]
            pltpu.make_async_copy(mine, mine, kv_sem.at[j]).wait()
            theirs = kall.at[j, :, block(2 + other)]
            pltpu.make_async_copy(theirs, theirs, xk_recv.at[j]).wait()
            window = kall.at[j, :, pl.ds(prompt, 2 * height)]
            pltpu.make_async_copy(window, window, win_recv.at[j]).wait()
            for i in range(2):
                gathered = pgath[i, :, :, cols(j, d)].astype(jnp.float32).reshape(prompt, d)
                kall[j, i, :prompt, :] = gathered.astype(jnp.bfloat16)

        near_far = pl.ds(pl.multiple_of(prompt + b * height, height), 3 * height)
        tri2 = twice(tri)
        keys = jnp.concatenate([kall[j, 0, :prompt], kall[j, 0, near_far]], axis=0)
        values = jnp.concatenate([kall[j, 1, :prompt], kall[j, 1, near_far]], axis=0)
        vt[...] = values.T
        for pair in range(group // 2):
            rows = slice(pair * 2 * height, (pair + 1) * 2 * height)
            scores = dot(keys, qs_t[s, j, :, rows])
            s_p = scores[:at1]
            s_n = scores[at2:at3] + twice(bias[b, 0])
            s_c = jnp.where(tri2, scores[at3:], scores[at1:at2]) + twice(bias[b, 1])
            top = jnp.maximum(
                jnp.maximum(jnp.max(s_p, axis=0, keepdims=True), jnp.max(s_n, axis=0, keepdims=True)),
                jnp.max(s_c, axis=0, keepdims=True),
            )
            e_p = jnp.exp2((s_p - top) * log_factor)
            e_n = jnp.exp2((s_n - top) * log_factor)
            e_c = jnp.exp2((s_c - top) * log_factor)
            total = (
                jnp.sum(e_p, axis=0, keepdims=True)
                + jnp.sum(e_n, axis=0, keepdims=True)
                + jnp.sum(e_c, axis=0, keepdims=True)
            )
            inv = 1.0 / total
            p_all[s, j, :at1, rows] = e_p.astype(jnp.bfloat16)
            p_all[s, j, at2:at3, rows] = e_n.astype(jnp.bfloat16)
            b_c = e_c.astype(jnp.bfloat16)
            b_d = b_c * twice(tri_b[...])
            p_all[s, j, at1:at2, rows] = b_c - b_d
            p_all[s, j, at3:, rows] = b_d
            out_t = (dot(vt[...], p_all[s, j, :, rows]) * inv).astype(jnp.bfloat16)
            cot_t = (cots_t[s, j, :, rows].astype(jnp.float32) * inv).astype(jnp.bfloat16)
            delta = jnp.sum(
                cot_t.astype(jnp.float32) * out_t.astype(jnp.float32), axis=0, keepdims=True
            )
            slopes = dot(values, cot_t)
            ds_all[s, j, :, rows] = (
                p_all[s, j, :, rows].astype(jnp.float32) * (slopes - delta)
            ).astype(jnp.bfloat16)
            cots[rows, :] = cot_t.T
            out = out_t.T
            for h in range(2):
                lanes = slice((2 * pair + h) * d, (2 * pair + h + 1) * d)
                attn[s, j, :, lanes] = out[h * height : (h + 1) * height]

        q_rows = jnp.concatenate([qog[s, j, 0, :, h * d : (h + 1) * d] for h in range(group)], axis=0)
        for i in range(2):
            part = dot(ds_all[s, j], q_rows) * factor if i == 0 else dot(p_all[s, j], cots[...])
            acc[j, i, :prompt] += part[:at1]
            acc[j, i, near_far] += part[at1:]

        @pl.when(s == 0)
        def _():
            out_copy(attn, j, at_send, at_recv).start()

        @pl.when(s == 1)
        def _():
            for i in range(2):
                psend[j, :, i] = acc[j, i, :prompt].reshape(n, own_prompt, d).astype(jnp.bfloat16)
                for t in range(2):
                    gsend[j, t, i] = acc[j, i, prompt + t * height : prompt + (t + 1) * height].astype(jnp.bfloat16)

            @pl.loop(1, n)
            def _(k):
                reduce_copy(j, k).start()

            pltpu.make_async_copy(psend.at[j, me], precv.at[core, j, chip], pr_recv.at[j]).start()
            for t in range(2):
                back_copy(j, t).start()
            sibling_copy(j).start()

    @pl.loop(0, 2 * half)
    def _(u):
        s = u // half
        j = lax.rem(u, half)
        b = s * core + (1 - s) * other
        near_far = pl.ds(pl.multiple_of(prompt + b * height, height), 3 * height)
        kt[:, :at1] = kall[j, 0, :prompt].T
        kt[:, at1:] = kall[j, 0, near_far].T
        dq_t = (dot(kt[...], ds_all[s, j]) * factor).astype(jnp.bfloat16)
        for h in range(group):
            rows = slice(h * height, (h + 1) * height)
            dq[s, j, :, rows] = dq_t[:, rows].T

        @pl.when(s == 0)
        def _():
            out_copy(dq, j, dq_send, dq_recv).start()

    for j in range(half):
        sibling_copy(j).wait_recv()
        back = grecv.at[:, j]
        pltpu.make_async_copy(back, back, gr_recv.at[j]).wait()
        for i, grad in enumerate((akg, avg)):
            mine = acc[j, i, block(2 + core)] + grecv[core, j, i].astype(jnp.float32)
            grad[:, cols(core * half + j, d)] = mine.astype(jnp.bfloat16)
            mine = srecv[j, i] + grecv[other, j, i].astype(jnp.float32)
            grad[:, cols(other * half + j, d)] = mine.astype(jnp.bfloat16)
    for j in range(half):
        terms = precv.at[:, j]
        pltpu.make_async_copy(terms, terms, pr_recv.at[j]).wait()
        for t in range(2):
            lanes = slice((t * half + j) * d, (t * half + j + 1) * d)
            for i, grad in enumerate((pkg, pvg)):
                grad[:, lanes] = jnp.sum(precv[t, j, :, i].astype(jnp.float32), axis=0)

    w_cross.wait_send()
    sent = pgath.at[:, pl.ds(0, n - 1)]
    pltpu.make_async_copy(sent, sent, pg_send).wait()
    for j in range(half):
        pltpu.make_async_copy(qog.at[1, j], qog.at[1, j], xq_send.at[j]).wait()
        mine = kall.at[j, :, block(2 + core)]
        pltpu.make_async_copy(mine, mine, xk_send.at[j]).wait()
        window = kall.at[j, :, pl.ds(prompt, 2 * height)]
        pltpu.make_async_copy(window, window, win_send.at[j]).wait()
        sent = psend.at[j, pl.ds(0, n - 1)]
        pltpu.make_async_copy(sent, sent, pr_send.at[j]).wait()
        pltpu.make_async_copy(gsend.at[j], gsend.at[j], gs_send.at[j]).wait()
        sibling_copy(j).wait_send()
        out_copy(attn, j, at_send, at_recv).wait()
        out_copy(dq, j, dq_send, dq_recv).wait()


def write_out(kv_heads, span, attn, dq, akg, avg, pkg, pvg, *refs):
    outs, (wide_sem, sem) = refs[:6], refs[6:]
    half = kv_heads // 2
    core = lax.rem(lax.axis_index("row"), 2)
    copies = [
        pltpu.make_async_copy(
            v.at[1 + t, j],
            out.at[:, pl.ds(pl.multiple_of((jnp.abs(core - t) * half + j) * span, span), span)],
            wide_sem.at[i, t, j],
        )
        for i, (v, out) in enumerate(((attn, outs[0]), (dq, outs[1])))
        for t in range(2)
        for j in range(half)
    ] + [
        pltpu.make_async_copy(v, out, sem.at[i])
        for i, (v, out) in enumerate(zip((akg, avg, pkg, pvg), outs[2:]))
    ]
    for copy in copies:
        copy.start()
    for copy in copies:
        copy.wait()


def per_device(n, queries, answer_keys, answer_values, prompt_keys, prompt_values, out_grad, weights, lengths):
    height = queries.shape[0]
    d = HEAD_DIM
    columns = answer_keys.shape[1]
    kv_heads = columns // d
    half = kv_heads // 2
    chips = n // 2
    group = queries.shape[1] // columns
    own_prompt = prompt_keys.shape[0]
    keys = own_prompt * n + 3 * height
    held = own_prompt * n + 4 * height
    span = group * d
    answers = lengths.shape[0]
    bf16, f32 = jnp.bfloat16, jnp.float32
    vmem = pl.BlockSpec(memory_space=pltpu.VMEM)
    hbm = pl.BlockSpec(memory_space=pltpu.HBM)
    dma = pltpu.SemaphoreType.DMA
    results = pl.pallas_call(
        functools.partial(kernel, n, kv_heads, group),
        out_shape=(
            pltpu.VMEM((3, half, height, span), bf16),
            pltpu.VMEM((3, half, height, span), bf16),
            pltpu.VMEM(answer_keys.shape, bf16),
            pltpu.VMEM(answer_keys.shape, bf16),
            pltpu.VMEM(prompt_keys.shape, f32),
            pltpu.VMEM(prompt_keys.shape, f32),
        ),
        in_specs=[hbm] * 8,
        out_specs=(vmem,) * 6,
        scratch_shapes=[
            pltpu.VMEM((2, half, 2, height, span), bf16),
            pltpu.VMEM((half, 2, held, d), bf16),
            pltpu.VMEM((d, keys), bf16),
            pltpu.VMEM((d, keys), bf16),
            pltpu.VMEM((2, n, own_prompt, half * d), bf16),
            pltpu.VMEM((2, 1, height), f32),
            pltpu.VMEM((1, answers), jnp.int32),
            pltpu.VMEM((2, half, d, group * height), bf16),
            pltpu.VMEM((group * height, d), bf16),
            pltpu.VMEM((2, half, d, group * height), bf16),
            pltpu.VMEM((2, half, keys, group * height), bf16),
            pltpu.VMEM((2, half, keys, group * height), bf16),
            pltpu.VMEM((half, 2, held, d), f32),
            pltpu.VMEM((half, n, 2, own_prompt, d), bf16),
            pltpu.VMEM((2, half, chips, 2, own_prompt, d), bf16),
            pltpu.VMEM((half, 2, 2, height, d), bf16),
            pltpu.VMEM((2, half, 2, height, d), bf16),
            pltpu.VMEM((half, 2, height, d), f32),
            pltpu.VMEM((2, 2, height, height), f32),
            pltpu.VMEM((height, height), bf16),
            dma((2,)),
            dma((half,)), dma((half,)), dma((half,)), dma((half,)), dma((half,)),
            dma,
            dma((half,)), dma((half,)), dma((half,)), dma((half,)), dma((half,)),
            dma,
            dma((half,)), dma((half,)), dma((half,)),
            dma,
            dma((half,)), dma((half,)), dma((half,)), dma((half,)), dma((half,)),
            dma, dma,
        ],
        compiler_params=pltpu.CompilerParams(
            collective_id=0, has_side_effects=True, vmem_limit_bytes=60 * 1024 * 1024
        ),
    )(
        queries, out_grad, answer_keys, answer_values, prompt_keys, prompt_values,
        weights.reshape(1, height), lengths.reshape(1, answers),
    )
    return pl.pallas_call(
        functools.partial(write_out, kv_heads, span),
        out_shape=(
            jax.ShapeDtypeStruct(queries.shape, bf16),
            jax.ShapeDtypeStruct(queries.shape, bf16),
            jax.ShapeDtypeStruct(answer_keys.shape, bf16),
            jax.ShapeDtypeStruct(answer_keys.shape, bf16),
            jax.ShapeDtypeStruct(prompt_keys.shape, f32),
            jax.ShapeDtypeStruct(prompt_keys.shape, f32),
        ),
        in_specs=[vmem] * 6,
        out_specs=(hbm,) * 6,
        scratch_shapes=[dma((2, 2, half)), dma((4,))],
        compiler_params=pltpu.CompilerParams(vmem_limit_bytes=8 * 1024 * 1024),
    )(*results)


def solution(mesh):
    both = ("grp", "row")
    wide = P(both, None)
    return jax.shard_map(
        functools.partial(per_device, mesh.shape["row"]),
        mesh=mesh,
        in_specs=(wide,) * 6 + (P(both), P("grp")),
        out_specs=(wide,) * 6,
        check_vma=False,
    )
```

time: 34.2 us -> 32.1 us (0.939)
  the two profiles are of different devices: /device:TPU:0 before, /device:TPU:3 now
where the time goes in v1:
time: 32.1 us; the launch traced here: 32 us
  Pallas kernels  31.3 us (98%)
  between operations  0.64 us (2%)
    pallas_call x1, Pallas kernels, per_device(): pl.pallas_call(functools.partial(kernel, n, kv_heads, group), out_shape=(...  29.8 us
    pallas_call x1, Pallas kernels, per_device(): pl.pallas_call(functools.partial(write_out, kv_heads, span), out_shape=(j...  1.52 us

profile of v1, /device:TPU:3, one launch (start us, length us, event | category | flops | bytes accessed | tf_op | source)
XLA Modules:
  0.0 32.0 jit_solution(10690209834441361755)
XLA Ops:
  0.6 29.8 %shard_map.127 = (bf16[3,2,128,1024]{3,2,1,0:T(8,128)(2,1)S(1)}, bf16[3,2,128,1024]{3,2,1,0:T(8,128)(2,1)S(1)}, bf16[128,512]{1,0:T(8,128)(2,1)S(1)}, bf16[128,5...) custom-call(bf16[128,4096]{1,0:T(8,128)(2,1)} %q_hbm.1, bf16[128,4096]{1,0:T(8,128)(2,1)} %og_hbm.1, ...), custom_call_target="tpu_custom_call" | custom-call | tf_op jit(solution)/shard_map/pallas_call | solution.py:382
  30.5 1.5 %shard_map.128 = (bf16[128,4096]{1,0:T(8,128)(2,1)}, bf16[128,4096]{1,0:T(8,128)(2,1)}, bf16[128,512]{1,0:T(8,128)(2,1)}, bf16[128,512]{1,0:T(8,128)(2,1)}, f32[8,512]{1,0:T(8,128)}, /*index=5*/f32[8,512]{1,0:T(8,128)}) custom-call(bf16[3,2,128,1024]{3,2,1,0:T(8,128)(2,1)S(1)} %get-tuple-element.12.attn, bf16[3,2,128,1024]{3,2,1,0:T(8,128)(2,1)S(1)} %get-tuple-element.13.dq, ...), custom_call_target="tpu_custom_call" | custom-call | tf_op jit(solution)/shard_map/pallas_call | solution.py:432

commit v2 on v1

--- a/solution.py
+++ b/solution.py
@@ -28,7 +28,7 @@
     qog, kall, vt, kt, pgath, wst, lst, qs_t, cots, cots_t, p_all, ds_all, acc,
     psend, precv, gsend, grecv, srecv, bias, tri_b,
     small_sem, in_sem, kv_sem, xq_recv, xk_recv, win_recv, pg_recv, pr_recv, gr_recv, sr_recv, at_recv, dq_recv,
-    xs_send, xq_send, xk_send, win_send, pg_send, pr_send, gs_send, sr_send, at_send, dq_send, w_recv, w_send,
+    xq_send, xk_send, win_send, pg_send, pr_send, gs_send, sr_send, at_send, dq_send, w_recv, w_send,
 ):
     me = lax.axis_index("row")
     height = ak.shape[0]
@@ -145,17 +145,31 @@
         for i in range(2):
             prompt_copy(k, i).start()
 
+    def send_window(j):
+        @pl.when(chip < chips - 1)
+        def _():
+            for copy in win_copies(j):
+                copy.start()
+
     w_cross = remote(w, wst.at[0], w_send, w_recv, sibling)
     w_cross.start()
-    for j in range(half):
-        for copy in win_copies(j):
-            copy.start()
+    send_window(0)
+    for j in range(half):
         for copy in cross_copies(j):
             copy.start()
         for copy in kv_cross(j):
             copy.start()
 
     acc[...] = jnp.zeros(acc.shape, jnp.float32)
+
+    @pl.when(chip == 0)
+    def _():
+        kall[:, :, prompt : prompt + 2 * height] = jnp.zeros((half, 2, 2 * height, d), jnp.bfloat16)
+
+    @pl.when(chip == chips - 1)
+    def _():
+        grecv[...] = jnp.zeros(grecv.shape, jnp.bfloat16)
+
     lens_local.wait()
     answers = lens.shape[1]
     row = lax.broadcasted_iota(jnp.int32, (answers, answers), 0)
@@ -198,6 +212,8 @@
         prepare(0, j)
 
     pltpu.make_async_copy(pgath, pgath, pg_recv).wait()
+    for j in range(1, half):
+        send_window(j)
 
     @pl.loop(0, 2 * half)
     def _(u):
@@ -211,8 +227,12 @@
             pltpu.make_async_copy(mine, mine, kv_sem.at[j]).wait()
             theirs = kall.at[j, :, block(2 + other)]
             pltpu.make_async_copy(theirs, theirs, xk_recv.at[j]).wait()
-            window = kall.at[j, :, pl.ds(prompt, 2 * height)]
-            pltpu.make_async_copy(window, window, win_recv.at[j]).wait()
+
+            @pl.when(chip > 0)
+            def _():
+                window = kall.at[j, :, pl.ds(prompt, 2 * height)]
+                pltpu.make_async_copy(window, window, win_recv.at[j]).wait()
+
             for i in range(2):
                 gathered = pgath[i, :, :, cols(j, d)].astype(jnp.float32).reshape(prompt, d)
                 kall[j, i, :prompt, :] = gathered.astype(jnp.bfloat16)
@@ -284,8 +304,12 @@
                 reduce_copy(j, k).start()
 
             pltpu.make_async_copy(psend.at[j, me], precv.at[core, j, chip], pr_recv.at[j]).start()
-            for t in range(2):
-                back_copy(j, t).start()
+
+            @pl.when(chip > 0)
+            def _():
+                for t in range(2):
+                    back_copy(j, t).start()
+
             sibling_copy(j).start()
 
     @pl.loop(0, 2 * half)
@@ -307,8 +331,12 @@
 
     for j in range(half):
         sibling_copy(j).wait_recv()
-        back = grecv.at[:, j]
-        pltpu.make_async_copy(back, back, gr_recv.at[j]).wait()
+
+        @pl.when(chip < chips - 1)
+        def _():
+            back = grecv.at[:, j]
+            pltpu.make_async_copy(back, back, gr_recv.at[j]).wait()
+
         for i, grad in enumerate((akg, avg)):
             mine = acc[j, i, block(2 + core)] + grecv[core, j, i].astype(jnp.float32)
             grad[:, cols(core * half + j, d)] = mine.astype(jnp.bfloat16)
@@ -329,11 +357,18 @@
         pltpu.make_async_copy(qog.at[1, j], qog.at[1, j], xq_send.at[j]).wait()
         mine = kall.at[j, :, block(2 + core)]
         pltpu.make_async_copy(mine, mine, xk_send.at[j]).wait()
-        window = kall.at[j, :, pl.ds(prompt, 2 * height)]
-        pltpu.make_async_copy(window, window, win_send.at[j]).wait()
+
+        @pl.when(chip < chips - 1)
+        def _():
+            window = kall.at[j, :, pl.ds(prompt, 2 * height)]
+            pltpu.make_async_copy(window, window, win_send.at[j]).wait()
+
+        @pl.when(chip > 0)
+        def _():
+            pltpu.make_async_copy(gsend.at[j], gsend.at[j], gs_send.at[j]).wait()
+
         sent = psend.at[j, pl.ds(0, n - 1)]
         pltpu.make_async_copy(sent, sent, pr_send.at[j]).wait()
-        pltpu.make_async_copy(gsend.at[j], gsend.at[j], gs_send.at[j]).wait()
         sibling_copy(j).wait_send()
         out_copy(attn, j, at_send, at_recv).wait()
         out_copy(dq, j, dq_send, dq_recv).wait()
@@ -416,7 +451,6 @@
             dma((half,)), dma((half,)), dma((half,)), dma((half,)), dma((half,)),
             dma,
             dma((half,)), dma((half,)), dma((half,)), dma((half,)), dma((half,)),
-            dma,
             dma((half,)), dma((half,)), dma((half,)),
             dma,
             dma((half,)), dma((half,)), dma((half,)), dma((half,)), dma((half,)),

time: 32.1 us -> 30.4 us (0.947)
  Pallas kernels: 31.3 us -> 29.6 us
    pallas_call x1, Pallas kernels: 29.8 us -> 28.1 us  [per_device(): pl.pallas_call(functools.partial(kernel, n, kv_heads, group), out_shape=(...]
where the time goes in v2:
time: 30.4 us; the launch traced here: 30.3 us
  Pallas kernels  29.6 us (97%)
  between operations  0.64 us (2%)
    pallas_call x1, Pallas kernels, per_device(): pl.pallas_call(functools.partial(kernel, n, kv_heads, group), out_shape=(...  28.1 us
    pallas_call x1, Pallas kernels, per_device(): pl.pallas_call(functools.partial(write_out, kv_heads, span), out_shape=(j...  1.52 us

profile of v2, /device:TPU:3, one launch (start us, length us, event | category | flops | bytes accessed | tf_op | source)
XLA Modules:
  0.0 30.3 jit_solution(18428551622594871655)
XLA Ops:
  0.6 28.1 %shard_map.127 = (bf16[3,2,128,1024]{3,2,1,0:T(8,128)(2,1)S(1)}, bf16[3,2,128,1024]{3,2,1,0:T(8,128)(2,1)S(1)}, bf16[128,512]{1,0:T(8,128)(2,1)S(1)}, bf16[128,5...) custom-call(bf16[128,4096]{1,0:T(8,128)(2,1)} %q_hbm.1, bf16[128,4096]{1,0:T(8,128)(2,1)} %og_hbm.1, ...), custom_call_target="tpu_custom_call" | custom-call | tf_op jit(solution)/shard_map/pallas_call | solution.py:417
  28.8 1.5 %shard_map.128 = (bf16[128,4096]{1,0:T(8,128)(2,1)}, bf16[128,4096]{1,0:T(8,128)(2,1)}, bf16[128,512]{1,0:T(8,128)(2,1)}, bf16[128,512]{1,0:T(8,128)(2,1)}, f32[8,512]{1,0:T(8,128)}, /*index=5*/f32[8,512]{1,0:T(8,128)}) custom-call(bf16[3,2,128,1024]{3,2,1,0:T(8,128)(2,1)S(1)} %get-tuple-element.12.attn, bf16[3,2,128,1024]{3,2,1,0:T(8,128)(2,1)S(1)} %get-tuple-element.13.dq, ...), custom_call_target="tpu_custom_call" | custom-call | tf_op jit(solution)/shard_map/pallas_call | solution.py:466

commit v3 on v2

--- a/solution.py
+++ b/solution.py
@@ -92,16 +92,16 @@
         return [
             remote(
                 src.at[:, pl.ds((t * half + j) * d, d)], kall.at[j, i, block(core)],
-                win_send.at[j], win_recv.at[j], 2 * after + t,
+                win_send.at[j], win_recv.at[j, core], 2 * after + t,
             )
             for i, src in enumerate((ak, av)) for t in range(2)
         ]
 
-    def prompt_copy(k, i):
+    def prompt_copy(j, k, i):
         target = lax.rem(me + k, n)
         return remote(
-            (pk, pv)[i].at[:, cols(lax.rem(target, 2), half * d)], pgath.at[i, me],
-            pg_send, pg_recv, target,
+            (pk, pv)[i].at[:, cols(lax.rem(target, 2) * half + j, d)], pgath.at[j, i, me],
+            pg_send.at[j], pg_recv.at[j], target,
         )
 
     def reduce_copy(j, k):
@@ -126,7 +126,9 @@
     w_local = pltpu.make_async_copy(w, wst.at[1], small_sem.at[0])
     lens_local = pltpu.make_async_copy(lens, lst, small_sem.at[1])
     own_prompts = [
-        pltpu.make_async_copy((pk, pv)[i].at[:, cols(core, half * d)], pgath.at[i, me], pg_recv) for i in range(2)
+        pltpu.make_async_copy((pk, pv)[i].at[:, cols(core * half + j, d)], pgath.at[j, i, me], pg_recv.at[j])
+        for j in range(half)
+        for i in range(2)
     ]
     w_local.start()
     lens_local.start()
@@ -140,21 +142,24 @@
         copy.start()
     pl.semaphore_wait(barrier, n - 1)
 
-    @pl.loop(1, n)
-    def _(k):
-        for i in range(2):
-            prompt_copy(k, i).start()
-
-    def send_window(j):
-        @pl.when(chip < chips - 1)
+    def send_prompts(j):
+        @pl.loop(1, n)
+        def _(k):
+            for i in range(2):
+                prompt_copy(j, k, i).start()
+
+    def send_window(j, condition):
+        @pl.when(jnp.logical_and(chip < chips - 1, condition))
         def _():
             for copy in win_copies(j):
                 copy.start()
 
     w_cross = remote(w, wst.at[0], w_send, w_recv, sibling)
     w_cross.start()
-    send_window(0)
     for j in range(half):
+        send_prompts(j)
+        if j == 0:
+            send_window(0, core == 1)
         for copy in cross_copies(j):
             copy.start()
         for copy in kv_cross(j):
@@ -204,6 +209,7 @@
         pltpu.make_async_copy(qog.at[1, j], qog.at[1, j], in_sem.at[j]).wait()
         prepare(1, j)
 
+    send_window(0, core == 0)
     w_cross.wait_recv()
 
     @pl.loop(0, half)
@@ -211,40 +217,48 @@
         pltpu.make_async_copy(qog.at[0, j], qog.at[0, j], xq_recv.at[j]).wait()
         prepare(0, j)
 
-    pltpu.make_async_copy(pgath, pgath, pg_recv).wait()
+    pltpu.make_async_copy(pgath.at[0], pgath.at[0], pg_recv.at[0]).wait()
     for j in range(1, half):
-        send_window(j)
+        send_window(j, True)
 
     @pl.loop(0, 2 * half)
     def _(u):
         j = u // 2
-        s = lax.rem(u, 2)
-        b = s * core + (1 - s) * other
-
-        @pl.when(s == 0)
+        b = 1 - lax.rem(u, 2)
+        s = b * core + (1 - b) * other
+
+        @pl.when(b == 1)
         def _():
             mine = kall.at[j, :, block(2 + core)]
             pltpu.make_async_copy(mine, mine, kv_sem.at[j]).wait()
             theirs = kall.at[j, :, block(2 + other)]
             pltpu.make_async_copy(theirs, theirs, xk_recv.at[j]).wait()
 
-            @pl.when(chip > 0)
+            @pl.when(j > 0)
             def _():
-                window = kall.at[j, :, pl.ds(prompt, 2 * height)]
-                pltpu.make_async_copy(window, window, win_recv.at[j]).wait()
+                pltpu.make_async_copy(pgath.at[j], pgath.at[j], pg_recv.at[j]).wait()
 
             for i in range(2):
-                gathered = pgath[i, :, :, cols(j, d)].astype(jnp.float32).reshape(prompt, d)
+                gathered = pgath[j, i].astype(jnp.float32).reshape(prompt, d)
                 kall[j, i, :prompt, :] = gathered.astype(jnp.bfloat16)
+
+        @pl.when(chip > 0)
+        def _():
+            window = kall.at[j, :, block(b)]
+            pltpu.make_async_copy(window, window, win_recv.at[j, b]).wait()
 
         near_far = pl.ds(pl.multiple_of(prompt + b * height, height), 3 * height)
         tri2 = twice(tri)
         keys = jnp.concatenate([kall[j, 0, :prompt], kall[j, 0, near_far]], axis=0)
         values = jnp.concatenate([kall[j, 1, :prompt], kall[j, 1, near_far]], axis=0)
         vt[...] = values.T
-        for pair in range(group // 2):
-            rows = slice(pair * 2 * height, (pair + 1) * 2 * height)
-            scores = dot(keys, qs_t[s, j, :, rows])
+        held = {}
+
+        def rows_of(pair):
+            return slice(pair * 2 * height, (pair + 1) * 2 * height)
+
+        def score(pair):
+            scores = dot(keys, qs_t[s, j, :, rows_of(pair)])
             s_p = scores[:at1]
             s_n = scores[at2:at3] + twice(bias[b, 0])
             s_c = jnp.where(tri2, scores[at3:], scores[at1:at2]) + twice(bias[b, 1])
@@ -252,6 +266,11 @@
                 jnp.maximum(jnp.max(s_p, axis=0, keepdims=True), jnp.max(s_n, axis=0, keepdims=True)),
                 jnp.max(s_c, axis=0, keepdims=True),
             )
+            held[pair] = s_p, s_n, s_c, top
+
+        def soften(pair):
+            rows = rows_of(pair)
+            s_p, s_n, s_c, top = held[pair]
             e_p = jnp.exp2((s_p - top) * log_factor)
             e_n = jnp.exp2((s_n - top) * log_factor)
             e_c = jnp.exp2((s_c - top) * log_factor)
@@ -260,27 +279,45 @@
                 + jnp.sum(e_n, axis=0, keepdims=True)
                 + jnp.sum(e_c, axis=0, keepdims=True)
             )
-            inv = 1.0 / total
             p_all[s, j, :at1, rows] = e_p.astype(jnp.bfloat16)
             p_all[s, j, at2:at3, rows] = e_n.astype(jnp.bfloat16)
             b_c = e_c.astype(jnp.bfloat16)
             b_d = b_c * twice(tri_b[...])
             p_all[s, j, at1:at2, rows] = b_c - b_d
             p_all[s, j, at3:, rows] = b_d
+            held[pair] = 1.0 / total
+
+        def attend(pair):
+            rows = rows_of(pair)
+            inv = held[pair]
             out_t = (dot(vt[...], p_all[s, j, :, rows]) * inv).astype(jnp.bfloat16)
             cot_t = (cots_t[s, j, :, rows].astype(jnp.float32) * inv).astype(jnp.bfloat16)
             delta = jnp.sum(
                 cot_t.astype(jnp.float32) * out_t.astype(jnp.float32), axis=0, keepdims=True
             )
-            slopes = dot(values, cot_t)
-            ds_all[s, j, :, rows] = (
-                p_all[s, j, :, rows].astype(jnp.float32) * (slopes - delta)
-            ).astype(jnp.bfloat16)
             cots[rows, :] = cot_t.T
             out = out_t.T
             for h in range(2):
                 lanes = slice((2 * pair + h) * d, (2 * pair + h + 1) * d)
                 attn[s, j, :, lanes] = out[h * height : (h + 1) * height]
+            held[pair] = cot_t, delta
+
+        def slope(pair):
+            rows = rows_of(pair)
+            cot_t, delta = held[pair]
+            slopes = dot(values, cot_t)
+            ds_all[s, j, :, rows] = p_all[s, j, :, rows] * (slopes - delta).astype(jnp.bfloat16)
+
+        pairs = group // 2
+        for step in range(-2, pairs + 2):
+            if 0 <= step < pairs:
+                soften(step)
+            if 0 <= step + 2 < pairs:
+                score(step + 2)
+            if 0 <= step - 1 < pairs:
+                attend(step - 1)
+            if 0 <= step - 2 < pairs:
+                slope(step - 2)
 
         q_rows = jnp.concatenate([qog[s, j, 0, :, h * d : (h + 1) * d] for h in range(group)], axis=0)
         for i in range(2):
@@ -292,7 +329,7 @@
         def _():
             out_copy(attn, j, at_send, at_recv).start()
 
-        @pl.when(s == 1)
+        @pl.when(b == 0)
         def _():
             for i in range(2):
                 psend[j, :, i] = acc[j, i, :prompt].reshape(n, own_prompt, d).astype(jnp.bfloat16)
@@ -351,9 +388,9 @@
                 grad[:, lanes] = jnp.sum(precv[t, j, :, i].astype(jnp.float32), axis=0)
 
     w_cross.wait_send()
-    sent = pgath.at[:, pl.ds(0, n - 1)]
-    pltpu.make_async_copy(sent, sent, pg_send).wait()
     for j in range(half):
+        sent = pgath.at[j, :, pl.ds(0, n - 1)]
+        pltpu.make_async_copy(sent, sent, pg_send.at[j]).wait()
         pltpu.make_async_copy(qog.at[1, j], qog.at[1, j], xq_send.at[j]).wait()
         mine = kall.at[j, :, block(2 + core)]
         pltpu.make_async_copy(mine, mine, xk_send.at[j]).wait()
@@ -431,7 +468,7 @@
             pltpu.VMEM((half, 2, held, d), bf16),
             pltpu.VMEM((d, keys), bf16),
             pltpu.VMEM((d, keys), bf16),
-            pltpu.VMEM((2, n, own_prompt, half * d), bf16),
+            pltpu.VMEM((half, 2, n, own_prompt, d), bf16),
             pltpu.VMEM((2, 1, height), f32),
             pltpu.VMEM((1, answers), jnp.int32),
             pltpu.VMEM((2, half, d, group * height), bf16),
@@ -448,12 +485,9 @@
             pltpu.VMEM((2, 2, height, height), f32),
             pltpu.VMEM((height, height), bf16),
             dma((2,)),
-            dma((half,)), dma((half,)), dma((half,)), dma((half,)), dma((half,)),
-            dma,
-            dma((half,)), dma((half,)), dma((half,)), dma((half,)), dma((half,)),
-            dma((half,)), dma((half,)), dma((half,)),
-            dma,
-            dma((half,)), dma((half,)), dma((half,)), dma((half,)), dma((half,)),
+            dma((half,)), dma((half,)), dma((half,)), dma((half,)),
+            dma((half, 2)),
+            *[dma((half,))] * 15,
             dma, dma,
         ],
         compiler_params=pltpu.CompilerParams(

time: 30.4 us -> 27.2 us (0.89)
  the two profiles are of different devices: /device:TPU:3 before, /device:TPU:1 now
where the time goes in v3:
time: 27.2 us; the launch traced here: 27.1 us
  Pallas kernels  26.4 us (97%)
  between operations  0.64 us (2%)
    pallas_call x1, Pallas kernels, per_device(): pl.pallas_call(functools.partial(kernel, n, kv_heads, group), out_shape=(...  24.9 us
    pallas_call x1, Pallas kernels, per_device(): pl.pallas_call(functools.partial(write_out, kv_heads, span), out_shape=(j...  1.52 us

profile of v3, /device:TPU:1, one launch (start us, length us, event | category | flops | bytes accessed | tf_op | source)
XLA Modules:
  0.0 27.1 jit_solution(6987881817259055318)
XLA Ops:
  0.6 24.9 %shard_map.127 = (bf16[3,2,128,1024]{3,2,1,0:T(8,128)(2,1)S(1)}, bf16[3,2,128,1024]{3,2,1,0:T(8,128)(2,1)S(1)}, bf16[128,512]{1,0:T(8,128)(2,1)S(1)}, bf16[128,5...) custom-call(bf16[128,4096]{1,0:T(8,128)(2,1)} %q_hbm.1, bf16[128,4096]{1,0:T(8,128)(2,1)} %og_hbm.1, ...), custom_call_target="tpu_custom_call" | custom-call | tf_op jit(solution)/shard_map/pallas_call | solution.py:454
  25.6 1.5 %shard_map.128 = (bf16[128,4096]{1,0:T(8,128)(2,1)}, bf16[128,4096]{1,0:T(8,128)(2,1)}, bf16[128,512]{1,0:T(8,128)(2,1)}, bf16[128,512]{1,0:T(8,128)(2,1)}, f32[8,512]{1,0:T(8,128)}, /*index=5*/f32[8,512]{1,0:T(8,128)}) custom-call(bf16[3,2,128,1024]{3,2,1,0:T(8,128)(2,1)S(1)} %get-tuple-element.12.attn, bf16[3,2,128,1024]{3,2,1,0:T(8,128)(2,1)S(1)} %get-tuple-element.13.dq, ...), custom_call_target="tpu_custom_call" | custom-call | tf_op jit(solution)/shard_map/pallas_call | solution.py:500

commit v4 on v3

--- a/solution.py
+++ b/solution.py
@@ -109,7 +109,15 @@
         return remote(psend.at[j, target], precv.at[core, j, chip], pr_send.at[j], pr_recv.at[j], target)
 
     def back_copy(j, t):
-        return remote(gsend.at[j, t], grecv.at[core, j], gs_send.at[j], gr_recv.at[j], 2 * before + t)
+        return remote(gsend.at[j, t], grecv.at[core, j], gs_send.at[j, t], gr_recv.at[j], 2 * before + t)
+
+    def send_back(j, t):
+        for i in range(2):
+            gsend[j, t, i] = acc[j, i, prompt + t * height : prompt + (t + 1) * height].astype(jnp.bfloat16)
+
+        @pl.when(chip > 0)
+        def _():
+            back_copy(j, t).start()
 
     def sibling_copy(j):
         return remote(acc.at[j, :, block(2 + other)], srecv.at[j], sr_send.at[j], sr_recv.at[j], sibling)
@@ -156,10 +164,9 @@
 
     w_cross = remote(w, wst.at[0], w_send, w_recv, sibling)
     w_cross.start()
-    for j in range(half):
-        send_prompts(j)
-        if j == 0:
-            send_window(0, core == 1)
+    send_prompts(0)
+    send_window(0, core == 1)
+    for j in range(half):
         for copy in cross_copies(j):
             copy.start()
         for copy in kv_cross(j):
@@ -217,37 +224,34 @@
         pltpu.make_async_copy(qog.at[0, j], qog.at[0, j], xq_recv.at[j]).wait()
         prepare(0, j)
 
+    for j in range(1, half):
+        send_prompts(j)
     pltpu.make_async_copy(pgath.at[0], pgath.at[0], pg_recv.at[0]).wait()
     for j in range(1, half):
         send_window(j, True)
 
-    @pl.loop(0, 2 * half)
-    def _(u):
-        j = u // 2
-        b = 1 - lax.rem(u, 2)
-        s = b * core + (1 - b) * other
-
-        @pl.when(b == 1)
-        def _():
+    def run_unit(j, b, leading):
+        s = core if b == 1 else other
+        if leading:
             mine = kall.at[j, :, block(2 + core)]
             pltpu.make_async_copy(mine, mine, kv_sem.at[j]).wait()
             theirs = kall.at[j, :, block(2 + other)]
             pltpu.make_async_copy(theirs, theirs, xk_recv.at[j]).wait()
-
-            @pl.when(j > 0)
-            def _():
+            if j > 0:
                 pltpu.make_async_copy(pgath.at[j], pgath.at[j], pg_recv.at[j]).wait()
-
             for i in range(2):
                 gathered = pgath[j, i].astype(jnp.float32).reshape(prompt, d)
                 kall[j, i, :prompt, :] = gathered.astype(jnp.bfloat16)
 
+        needed = ((0,) if b == 0 else ()) + ((1,) if leading else ())
+
         @pl.when(chip > 0)
         def _():
-            window = kall.at[j, :, block(b)]
-            pltpu.make_async_copy(window, window, win_recv.at[j, b]).wait()
-
-        near_far = pl.ds(pl.multiple_of(prompt + b * height, height), 3 * height)
+            for t in needed:
+                window = kall.at[j, :, block(t)]
+                pltpu.make_async_copy(window, window, win_recv.at[j, t]).wait()
+
+        near_far = slice(prompt + b * height, prompt + (b + 3) * height)
         tri2 = twice(tri)
         keys = jnp.concatenate([kall[j, 0, :prompt], kall[j, 0, near_far]], axis=0)
         values = jnp.concatenate([kall[j, 1, :prompt], kall[j, 1, near_far]], axis=0)
@@ -295,7 +299,7 @@
             delta = jnp.sum(
                 cot_t.astype(jnp.float32) * out_t.astype(jnp.float32), axis=0, keepdims=True
             )
-            cots[rows, :] = cot_t.T
+            cots[s, j, rows, :] = cot_t.T
             out = out_t.T
             for h in range(2):
                 lanes = slice((2 * pair + h) * d, (2 * pair + h + 1) * d)
@@ -319,35 +323,39 @@
             if 0 <= step - 2 < pairs:
                 slope(step - 2)
 
+        key_terms(j, b, slice(0, at3 if b == 0 else at2))
+
+        @pl.when(s == 0)
+        def _():
+            out_copy(attn, j, at_send, at_recv).start()
+
+    def key_terms(j, b, rows):
+        s = core if b == 1 else other
         q_rows = jnp.concatenate([qog[s, j, 0, :, h * d : (h + 1) * d] for h in range(group)], axis=0)
+        start = max(rows.start, at1)
+        window = slice(start + b * height, rows.stop + b * height)
         for i in range(2):
-            part = dot(ds_all[s, j], q_rows) * factor if i == 0 else dot(p_all[s, j], cots[...])
-            acc[j, i, :prompt] += part[:at1]
-            acc[j, i, near_far] += part[at1:]
-
-        @pl.when(s == 0)
-        def _():
-            out_copy(attn, j, at_send, at_recv).start()
-
-        @pl.when(b == 0)
-        def _():
-            for i in range(2):
-                psend[j, :, i] = acc[j, i, :prompt].reshape(n, own_prompt, d).astype(jnp.bfloat16)
-                for t in range(2):
-                    gsend[j, t, i] = acc[j, i, prompt + t * height : prompt + (t + 1) * height].astype(jnp.bfloat16)
-
-            @pl.loop(1, n)
-            def _(k):
-                reduce_copy(j, k).start()
-
-            pltpu.make_async_copy(psend.at[j, me], precv.at[core, j, chip], pr_recv.at[j]).start()
-
-            @pl.when(chip > 0)
-            def _():
-                for t in range(2):
-                    back_copy(j, t).start()
-
-            sibling_copy(j).start()
+            part = dot(ds_all[s, j, rows], q_rows) * factor if i == 0 else dot(p_all[s, j, rows], cots[s, j])
+            if rows.start == 0:
+                acc[j, i, :prompt] += part[:at1]
+            acc[j, i, window] += part[start - rows.start :]
+
+    for j in range(half):
+        for place, b in enumerate((1, 0) if j == 0 else (0, 1)):
+            run_unit(j, b, place == 0)
+            if j > 0 and b == 0:
+                send_back(j, 0)
+        for i in range(2):
+            psend[j, :, i] = acc[j, i, :prompt].reshape(n, own_prompt, d).astype(jnp.bfloat16)
+
+        @pl.loop(1, n)
+        def _(k):
+            reduce_copy(j, k).start()
+
+        pltpu.make_async_copy(psend.at[j, me], precv.at[core, j, chip], pr_recv.at[j]).start()
+        if j == 0:
+            send_back(j, 0)
+        send_back(j, 1)
 
     @pl.loop(0, 2 * half)
     def _(u):
@@ -367,6 +375,11 @@
             out_copy(dq, j, dq_send, dq_recv).start()
 
     for j in range(half):
+        key_terms(j, 0, slice(at3, at3 + height))
+        key_terms(j, 1, slice(at2, at3 + height))
+        sibling_copy(j).start()
+
+    for j in range(half):
         sibling_copy(j).wait_recv()
 
         @pl.when(chip < chips - 1)
@@ -402,7 +415,8 @@
 
         @pl.when(chip > 0)
         def _():
-            pltpu.make_async_copy(gsend.at[j], gsend.at[j], gs_send.at[j]).wait()
+            for t in range(2):
+                back_copy(j, t).wait_send()
 
         sent = psend.at[j, pl.ds(0, n - 1)]
         pltpu.make_async_copy(sent, sent, pr_send.at[j]).wait()
@@ -472,7 +486,7 @@
             pltpu.VMEM((2, 1, height), f32),
             pltpu.VMEM((1, answers), jnp.int32),
             pltpu.VMEM((2, half, d, group * height), bf16),
-            pltpu.VMEM((group * height, d), bf16),
+            pltpu.VMEM((2, half, group * height, d), bf16),
             pltpu.VMEM((2, half, d, group * height), bf16),
             pltpu.VMEM((2, half, keys, group * height), bf16),
             pltpu.VMEM((2, half, keys, group * height), bf16),
@@ -487,7 +501,9 @@
             dma((2,)),
             dma((half,)), dma((half,)), dma((half,)), dma((half,)),
             dma((half, 2)),
-            *[dma((half,))] * 15,
+            *[dma((half,))] * 11,
+            dma((half, 2)),
+            *[dma((half,))] * 3,
             dma, dma,
         ],
         compiler_params=pltpu.CompilerParams(

time: 27.2 us -> 26.7 us (0.982)
  the two profiles are of different devices: /device:TPU:1 before, /device:TPU:0 now
where the time goes in v4:
time: 26.7 us; the launch traced here: 26.6 us
  Pallas kernels  25.9 us (97%)
  between operations  0.64 us (2%)
    pallas_call x1, Pallas kernels, per_device(): pl.pallas_call(functools.partial(kernel, n, kv_heads, group), out_shape=(...  24.4 us
    pallas_call x1, Pallas kernels, per_device(): pl.pallas_call(functools.partial(write_out, kv_heads, span), out_shape=(j...  1.52 us

profile of v4, /device:TPU:0, one launch (start us, length us, event | category | flops | bytes accessed | tf_op | source)
XLA Modules:
  0.0 26.6 jit_solution(9654629248583749781)
XLA Ops:
  0.6 24.4 %shard_map.127 = (bf16[3,2,128,1024]{3,2,1,0:T(8,128)(2,1)S(1)}, bf16[3,2,128,1024]{3,2,1,0:T(8,128)(2,1)S(1)}, bf16[128,512]{1,0:T(8,128)(2,1)S(1)}, bf16[128,5...) custom-call(bf16[128,4096]{1,0:T(8,128)(2,1)} %q_hbm.1, bf16[128,4096]{1,0:T(8,128)(2,1)} %og_hbm.1, ...), custom_call_target="tpu_custom_call" | custom-call | tf_op jit(solution)/shard_map/pallas_call | solution.py:468
  25.1 1.5 %shard_map.128 = (bf16[128,4096]{1,0:T(8,128)(2,1)}, bf16[128,4096]{1,0:T(8,128)(2,1)}, bf16[128,512]{1,0:T(8,128)(2,1)}, bf16[128,512]{1,0:T(8,128)(2,1)}, f32[8,512]{1,0:T(8,128)}, /*index=5*/f32[8,512]{1,0:T(8,128)}) custom-call(bf16[3,2,128,1024]{3,2,1,0:T(8,128)(2,1)S(1)} %get-tuple-element.12.attn, bf16[3,2,128,1024]{3,2,1,0:T(8,128)(2,1)S(1)} %get-tuple-element.13.dq, ...), custom_call_target="tpu_custom_call" | custom-call | tf_op jit(solution)/shard_map/pallas_call | solution.py:516

commit v5 on v4

--- a/solution.py
+++ b/solution.py
@@ -88,36 +88,47 @@
             for i, src in enumerate((ak, av))
         ]
 
-    def win_copies(j):
-        return [
-            remote(
-                src.at[:, pl.ds((t * half + j) * d, d)], kall.at[j, i, block(core)],
-                win_send.at[j], win_recv.at[j, core], 2 * after + t,
-            )
-            for i, src in enumerate((ak, av)) for t in range(2)
-        ]
+    def win_copy(j, i, t):
+        return remote(
+            (ak, av)[i].at[:, pl.ds((t * half + j) * d, d)], kall.at[j, i, block(core)],
+            win_send.at[j], win_recv.at[j, core, i], 2 * after + t,
+        )
 
     def prompt_copy(j, k, i):
         target = lax.rem(me + k, n)
         return remote(
             (pk, pv)[i].at[:, cols(lax.rem(target, 2) * half + j, d)], pgath.at[j, i, me],
-            pg_send.at[j], pg_recv.at[j], target,
-        )
-
-    def reduce_copy(j, k):
+            pg_send.at[j], pg_recv.at[j, i], target,
+        )
+
+    def reduce_copy(j, k, part):
         target = lax.rem(me + k, n)
-        return remote(psend.at[j, target], precv.at[core, j, chip], pr_send.at[j], pr_recv.at[j], target)
-
-    def back_copy(j, t):
-        return remote(gsend.at[j, t], grecv.at[core, j], gs_send.at[j, t], gr_recv.at[j], 2 * before + t)
-
-    def send_back(j, t):
-        for i in range(2):
+        return remote(
+            psend.at[j, part, target], precv.at[core, j, part, chip], pr_send.at[j], pr_recv.at[j], target
+        )
+
+    def send_reduce(j, part):
+        for i in range(part.start, part.start + part.size):
+            psend[j, i] = acc[j, i, :prompt].reshape(n, own_prompt, d).astype(jnp.bfloat16)
+
+        @pl.loop(1, n)
+        def _(k):
+            reduce_copy(j, k, part).start()
+
+        pltpu.make_async_copy(psend.at[j, part, me], precv.at[core, j, part, chip], pr_recv.at[j]).start()
+
+    def back_copy(j, t, part):
+        return remote(
+            gsend.at[j, t, part], grecv.at[core, j, part], gs_send.at[j, t], gr_recv.at[j], 2 * before + t
+        )
+
+    def send_back(j, t, part):
+        for i in range(part.start, part.start + part.size):
             gsend[j, t, i] = acc[j, i, prompt + t * height : prompt + (t + 1) * height].astype(jnp.bfloat16)
 
         @pl.when(chip > 0)
         def _():
-            back_copy(j, t).start()
+            back_copy(j, t, part).start()
 
     def sibling_copy(j):
         return remote(acc.at[j, :, block(2 + other)], srecv.at[j], sr_send.at[j], sr_recv.at[j], sibling)
@@ -134,7 +145,7 @@
     w_local = pltpu.make_async_copy(w, wst.at[1], small_sem.at[0])
     lens_local = pltpu.make_async_copy(lens, lst, small_sem.at[1])
     own_prompts = [
-        pltpu.make_async_copy((pk, pv)[i].at[:, cols(core * half + j, d)], pgath.at[j, i, me], pg_recv.at[j])
+        pltpu.make_async_copy((pk, pv)[i].at[:, cols(core * half + j, d)], pgath.at[j, i, me], pg_recv.at[j, i])
         for j in range(half)
         for i in range(2)
     ]
@@ -150,22 +161,22 @@
         copy.start()
     pl.semaphore_wait(barrier, n - 1)
 
-    def send_prompts(j):
+    def send_prompts(j, i):
         @pl.loop(1, n)
         def _(k):
-            for i in range(2):
-                prompt_copy(j, k, i).start()
-
-    def send_window(j, condition):
+            prompt_copy(j, k, i).start()
+
+    def send_window(j, i, condition):
         @pl.when(jnp.logical_and(chip < chips - 1, condition))
         def _():
-            for copy in win_copies(j):
-                copy.start()
+            for t in range(2):
+                win_copy(j, i, t).start()
 
     w_cross = remote(w, wst.at[0], w_send, w_recv, sibling)
     w_cross.start()
-    send_prompts(0)
-    send_window(0, core == 1)
+    for i in range(2):
+        send_prompts(0, i)
+        send_window(0, i, core == 1)
     for j in range(half):
         for copy in cross_copies(j):
             copy.start()
@@ -216,7 +227,8 @@
         pltpu.make_async_copy(qog.at[1, j], qog.at[1, j], in_sem.at[j]).wait()
         prepare(1, j)
 
-    send_window(0, core == 0)
+    for i in range(2):
+        send_window(0, i, core == 0)
     w_cross.wait_recv()
 
     @pl.loop(0, half)
@@ -225,10 +237,28 @@
         prepare(0, j)
 
     for j in range(1, half):
-        send_prompts(j)
-    pltpu.make_async_copy(pgath.at[0], pgath.at[0], pg_recv.at[0]).wait()
+        for i in range(2):
+            send_prompts(j, i)
+    pltpu.make_async_copy(pgath.at[0, 0], pgath.at[0, 0], pg_recv.at[0, 0]).wait()
     for j in range(1, half):
-        send_window(j, True)
+        for i in range(2):
+            send_window(j, i, True)
+
+    def assemble(j, i):
+        if j > 0 or i > 0:
+            pltpu.make_async_copy(pgath.at[j, i], pgath.at[j, i], pg_recv.at[j, i]).wait()
+        gathered = pgath[j, i].astype(jnp.float32).reshape(prompt, d)
+        kall[j, i, :prompt, :] = gathered.astype(jnp.bfloat16)
+
+    def arrive(j, i, b, leading):
+        if leading:
+            assemble(j, i)
+
+        @pl.when(chip > 0)
+        def _():
+            for t in ((0,) if b == 0 else ()) + ((1,) if leading else ()):
+                window = kall.at[j, i, block(t)]
+                pltpu.make_async_copy(window, window, win_recv.at[j, t, i]).wait()
 
     def run_unit(j, b, leading):
         s = core if b == 1 else other
@@ -237,25 +267,20 @@
             pltpu.make_async_copy(mine, mine, kv_sem.at[j]).wait()
             theirs = kall.at[j, :, block(2 + other)]
             pltpu.make_async_copy(theirs, theirs, xk_recv.at[j]).wait()
-            if j > 0:
-                pltpu.make_async_copy(pgath.at[j], pgath.at[j], pg_recv.at[j]).wait()
-            for i in range(2):
-                gathered = pgath[j, i].astype(jnp.float32).reshape(prompt, d)
-                kall[j, i, :prompt, :] = gathered.astype(jnp.bfloat16)
-
-        needed = ((0,) if b == 0 else ()) + ((1,) if leading else ())
-
-        @pl.when(chip > 0)
-        def _():
-            for t in needed:
-                window = kall.at[j, :, block(t)]
-                pltpu.make_async_copy(window, window, win_recv.at[j, t]).wait()
+        arrive(j, 0, b, leading)
+        late = leading and j == 0
+        if not late:
+            arrive(j, 1, b, leading)
 
         near_far = slice(prompt + b * height, prompt + (b + 3) * height)
         tri2 = twice(tri)
         keys = jnp.concatenate([kall[j, 0, :prompt], kall[j, 0, near_far]], axis=0)
-        values = jnp.concatenate([kall[j, 1, :prompt], kall[j, 1, near_far]], axis=0)
-        vt[...] = values.T
+
+        def values():
+            return jnp.concatenate([kall[j, 1, :prompt], kall[j, 1, near_far]], axis=0)
+
+        if not late:
+            vt[...] = values().T
         held = {}
 
         def rows_of(pair):
@@ -309,53 +334,52 @@
         def slope(pair):
             rows = rows_of(pair)
             cot_t, delta = held[pair]
-            slopes = dot(values, cot_t)
+            slopes = dot(values(), cot_t)
             ds_all[s, j, :, rows] = p_all[s, j, :, rows] * (slopes - delta).astype(jnp.bfloat16)
 
         pairs = group // 2
+        rows = slice(0, at3 if b == 0 else at2)
         for step in range(-2, pairs + 2):
             if 0 <= step < pairs:
                 soften(step)
             if 0 <= step + 2 < pairs:
                 score(step + 2)
+            if late and step == 0:
+                arrive(j, 1, b, leading)
+                vt[...] = values().T
             if 0 <= step - 1 < pairs:
                 attend(step - 1)
             if 0 <= step - 2 < pairs:
                 slope(step - 2)
 
-        key_terms(j, b, slice(0, at3 if b == 0 else at2))
-
+        key_terms(j, b, 0, rows)
+        key_terms(j, b, 1, rows)
         @pl.when(s == 0)
         def _():
             out_copy(attn, j, at_send, at_recv).start()
 
-    def key_terms(j, b, rows):
+    def key_terms(j, b, i, rows):
         s = core if b == 1 else other
-        q_rows = jnp.concatenate([qog[s, j, 0, :, h * d : (h + 1) * d] for h in range(group)], axis=0)
         start = max(rows.start, at1)
         window = slice(start + b * height, rows.stop + b * height)
-        for i in range(2):
-            part = dot(ds_all[s, j, rows], q_rows) * factor if i == 0 else dot(p_all[s, j, rows], cots[s, j])
-            if rows.start == 0:
-                acc[j, i, :prompt] += part[:at1]
-            acc[j, i, window] += part[start - rows.start :]
+        if i == 0:
+            q_rows = jnp.concatenate([qog[s, j, 0, :, h * d : (h + 1) * d] for h in range(group)], axis=0)
+            part = dot(ds_all[s, j, rows], q_rows) * factor
+        else:
+            part = dot(p_all[s, j, rows], cots[s, j])
+        if rows.start == 0:
+            acc[j, i, :prompt] += part[:at1]
+        acc[j, i, window] += part[start - rows.start :]
 
     for j in range(half):
         for place, b in enumerate((1, 0) if j == 0 else (0, 1)):
             run_unit(j, b, place == 0)
             if j > 0 and b == 0:
-                send_back(j, 0)
-        for i in range(2):
-            psend[j, :, i] = acc[j, i, :prompt].reshape(n, own_prompt, d).astype(jnp.bfloat16)
-
-        @pl.loop(1, n)
-        def _(k):
-            reduce_copy(j, k).start()
-
-        pltpu.make_async_copy(psend.at[j, me], precv.at[core, j, chip], pr_recv.at[j]).start()
+                send_back(j, 0, pl.ds(0, 2))
+        send_reduce(j, pl.ds(0, 2))
         if j == 0:
-            send_back(j, 0)
-        send_back(j, 1)
+            send_back(j, 0, pl.ds(0, 2))
+        send_back(j, 1, pl.ds(0, 2))
 
     @pl.loop(0, 2 * half)
     def _(u):
@@ -375,8 +399,9 @@
             out_copy(dq, j, dq_send, dq_recv).start()
 
     for j in range(half):
-        key_terms(j, 0, slice(at3, at3 + height))
-        key_terms(j, 1, slice(at2, at3 + height))
+        for i in range(2):
+            key_terms(j, 0, i, slice(at3, at3 + height))
+            key_terms(j, 1, i, slice(at2, at3 + height))
         sibling_copy(j).start()
 
     for j in range(half):
@@ -398,7 +423,7 @@
         for t in range(2):
             lanes = slice((t * half + j) * d, (t * half + j + 1) * d)
             for i, grad in enumerate((pkg, pvg)):
-                grad[:, lanes] = jnp.sum(precv[t, j, :, i].astype(jnp.float32), axis=0)
+                grad[:, lanes] = jnp.sum(precv[t, j, i].astype(jnp.float32), axis=0)
 
     w_cross.wait_send()
     for j in range(half):
@@ -416,9 +441,9 @@
         @pl.when(chip > 0)
         def _():
             for t in range(2):
-                back_copy(j, t).wait_send()
-
-        sent = psend.at[j, pl.ds(0, n - 1)]
+                back_copy(j, t, pl.ds(0, 2)).wait_send()
+
+        sent = psend.at[j, :, pl.ds(0, n - 1)]
         pltpu.make_async_copy(sent, sent, pr_send.at[j]).wait()
         sibling_copy(j).wait_send()
         out_copy(attn, j, at_send, at_recv).wait()
@@ -491,8 +516,8 @@
             pltpu.VMEM((2, half, keys, group * height), bf16),
             pltpu.VMEM((2, half, keys, group * height), bf16),
             pltpu.VMEM((half, 2, held, d), f32),
-            pltpu.VMEM((half, n, 2, own_prompt, d), bf16),
-            pltpu.VMEM((2, half, chips, 2, own_prompt, d), bf16),
+            pltpu.VMEM((half, 2, n, own_prompt, d), bf16),
+            pltpu.VMEM((2, half, 2, chips, own_prompt, d), bf16),
             pltpu.VMEM((half, 2, 2, height, d), bf16),
             pltpu.VMEM((2, half, 2, height, d), bf16),
             pltpu.VMEM((half, 2, height, d), f32),
@@ -500,8 +525,9 @@
             pltpu.VMEM((height, height), bf16),
             dma((2,)),
             dma((half,)), dma((half,)), dma((half,)), dma((half,)),
+            dma((half, 2, 2)),
             dma((half, 2)),
-            *[dma((half,))] * 11,
+            *[dma((half,))] * 10,
             dma((half, 2)),
             *[dma((half,))] * 3,
             dma, dma,

time: 26.7 us -> 26.2 us (0.981)
  Pallas kernels: 25.9 us -> 25.4 us
    pallas_call x1, Pallas kernels: 24.4 us -> 23.9 us  [per_device(): pl.pallas_call(functools.partial(kernel, n, kv_heads, group), out_shape=(...]
where the time goes in v5:
time: 26.2 us; the launch traced here: 26 us
  Pallas kernels  25.4 us (97%)
  between operations  0.64 us (2%)
    pallas_call x1, Pallas kernels, per_device(): pl.pallas_call(functools.partial(kernel, n, kv_heads, group), out_shape=(...  23.9 us
    pallas_call x1, Pallas kernels, per_device(): pl.pallas_call(functools.partial(write_out, kv_heads, span), out_shape=(j...  1.52 us

profile of v5, /device:TPU:0, one launch (start us, length us, event | category | flops | bytes accessed | tf_op | source)
XLA Modules:
  0.0 26.0 jit_solution(3903966440271436757)
XLA Ops:
  0.6 23.9 %shard_map.127 = (bf16[3,2,128,1024]{3,2,1,0:T(8,128)(2,1)S(1)}, bf16[3,2,128,1024]{3,2,1,0:T(8,128)(2,1)S(1)}, bf16[128,512]{1,0:T(8,128)(2,1)S(1)}, bf16[128,5...) custom-call(bf16[128,4096]{1,0:T(8,128)(2,1)} %q_hbm.1, bf16[128,4096]{1,0:T(8,128)(2,1)} %og_hbm.1, ...), custom_call_target="tpu_custom_call" | custom-call | tf_op jit(solution)/shard_map/pallas_call | solution.py:493
  24.5 1.5 %shard_map.128 = (bf16[128,4096]{1,0:T(8,128)(2,1)}, bf16[128,4096]{1,0:T(8,128)(2,1)}, bf16[128,512]{1,0:T(8,128)(2,1)}, bf16[128,512]{1,0:T(8,128)(2,1)}, f32[8,512]{1,0:T(8,128)}, /*index=5*/f32[8,512]{1,0:T(8,128)}) custom-call(bf16[3,2,128,1024]{3,2,1,0:T(8,128)(2,1)S(1)} %get-tuple-element.12.attn, bf16[3,2,128,1024]{3,2,1,0:T(8,128)(2,1)S(1)} %get-tuple-element.13.dq, ...), custom_call_target="tpu_custom_call" | custom-call | tf_op jit(solution)/shard_map/pallas_call | solution.py:542

commit v6 on v5

--- a/solution.py
+++ b/solution.py
@@ -26,9 +26,9 @@
     q_hbm, og_hbm, ak, av, pk, pv, w, lens,
     attn, dq, akg, avg, pkg, pvg,
     qog, kall, vt, kt, pgath, wst, lst, qs_t, cots, cots_t, p_all, ds_all, acc,
-    psend, precv, gsend, grecv, srecv, bias, tri_b,
+    psend, precv, gsend, grecv, srecv, bias, tri_b, deltas,
     small_sem, in_sem, kv_sem, xq_recv, xk_recv, win_recv, pg_recv, pr_recv, gr_recv, sr_recv, at_recv, dq_recv,
-    xq_send, xk_send, win_send, pg_send, pr_send, gs_send, sr_send, at_send, dq_send, w_recv, w_send,
+    xq_send, xk_send, win_send, pg_send, pr_send, gs_send, sr_send, at_send, dq_send, w_recv, w_send, go,
 ):
     me = lax.axis_index("row")
     height = ak.shape[0]
@@ -138,9 +138,26 @@
 
     barrier = pltpu.get_barrier_semaphore()
 
-    @pl.loop(1, n)
-    def _(k):
-        pl.semaphore_signal(barrier, inc=1, device_id={"row": lax.rem(me + k, n)}, device_id_type=MESH)
+    def signal(semaphore, target):
+        pl.semaphore_signal(semaphore, inc=1, device_id={"row": target}, device_id_type=MESH)
+
+    collector = n - 2
+
+    @pl.when(me < n - 4)
+    def _():
+        signal(barrier, collector)
+
+    @pl.when(chip > 0)
+    def _():
+        for t in range(2):
+            signal(barrier, 2 * before + t)
+
+    @pl.when(chip < chips - 1)
+    def _():
+        for t in range(2):
+            signal(barrier, 2 * after + t)
+
+    signal(barrier, sibling)
 
     w_local = pltpu.make_async_copy(w, wst.at[1], small_sem.at[0])
     lens_local = pltpu.make_async_copy(lens, lst, small_sem.at[1])
@@ -159,7 +176,20 @@
             copy.start()
     for copy in own_prompts:
         copy.start()
-    pl.semaphore_wait(barrier, n - 1)
+    @pl.when(me == collector)
+    def _():
+        pl.semaphore_wait(barrier, n - 1)
+
+        @pl.loop(1, n)
+        def _(k):
+            signal(go, lax.rem(me + k, n))
+
+    @pl.when(me != collector)
+    def _():
+        pl.semaphore_wait(
+            barrier, 1 + 2 * (chip > 0).astype(jnp.int32) + 2 * (chip < chips - 1).astype(jnp.int32)
+        )
+
 
     def send_prompts(j, i):
         @pl.loop(1, n)
@@ -175,13 +205,21 @@
     w_cross = remote(w, wst.at[0], w_send, w_recv, sibling)
     w_cross.start()
     for i in range(2):
-        send_prompts(0, i)
         send_window(0, i, core == 1)
+    send_window(0, 0, core == 0)
     for j in range(half):
         for copy in cross_copies(j):
             copy.start()
         for copy in kv_cross(j):
             copy.start()
+
+    @pl.when(me != collector)
+    def _():
+        pl.semaphore_wait(go, 1)
+
+    for i in range(2):
+        send_prompts(0, i)
+    send_window(0, 1, core == 0)
 
     acc[...] = jnp.zeros(acc.shape, jnp.float32)
 
@@ -227,8 +265,9 @@
         pltpu.make_async_copy(qog.at[1, j], qog.at[1, j], in_sem.at[j]).wait()
         prepare(1, j)
 
-    for i in range(2):
-        send_window(0, i, core == 0)
+    for j in range(1, half):
+        for i in range(2):
+            send_prompts(j, i)
     w_cross.wait_recv()
 
     @pl.loop(0, half)
@@ -238,11 +277,8 @@
 
     for j in range(1, half):
         for i in range(2):
-            send_prompts(j, i)
+            send_window(j, i, True)
     pltpu.make_async_copy(pgath.at[0, 0], pgath.at[0, 0], pg_recv.at[0, 0]).wait()
-    for j in range(1, half):
-        for i in range(2):
-            send_window(j, i, True)
 
     def assemble(j, i):
         if j > 0 or i > 0:
@@ -324,6 +360,8 @@
             delta = jnp.sum(
                 cot_t.astype(jnp.float32) * out_t.astype(jnp.float32), axis=0, keepdims=True
             )
+            cots_t[s, j, :, rows] = cot_t
+            deltas[s, j, :, rows] = delta
             cots[s, j, rows, :] = cot_t.T
             out = out_t.T
             for h in range(2):
@@ -331,14 +369,15 @@
                 attn[s, j, :, lanes] = out[h * height : (h + 1) * height]
             held[pair] = cot_t, delta
 
+        rows = slice(0, at3 if b == 0 else at2)
+
         def slope(pair):
-            rows = rows_of(pair)
+            lanes = rows_of(pair)
             cot_t, delta = held[pair]
-            slopes = dot(values(), cot_t)
-            ds_all[s, j, :, rows] = p_all[s, j, :, rows] * (slopes - delta).astype(jnp.bfloat16)
+            slopes = dot(values()[rows], cot_t)
+            ds_all[s, j, rows, lanes] = p_all[s, j, rows, lanes] * (slopes - delta).astype(jnp.bfloat16)
 
         pairs = group // 2
-        rows = slice(0, at3 if b == 0 else at2)
         for step in range(-2, pairs + 2):
             if 0 <= step < pairs:
                 soften(step)
@@ -371,6 +410,20 @@
             acc[j, i, :prompt] += part[:at1]
         acc[j, i, window] += part[start - rows.start :]
 
+    def local_rows(b):
+        return slice(at3 if b == 0 else at2, at3 + height)
+
+    def local_slope(j, b):
+        s = core if b == 1 else other
+        rows = local_rows(b)
+        values = kall[j, 1, rows.start + b * height : rows.stop + b * height]
+        for pair in range(group // 2):
+            lanes = slice(pair * 2 * height, (pair + 1) * 2 * height)
+            slopes = dot(values, cots_t[s, j, :, lanes])
+            ds_all[s, j, rows, lanes] = p_all[s, j, rows, lanes] * (
+                slopes - deltas[s, j, :, lanes]
+            ).astype(jnp.bfloat16)
+
     for j in range(half):
         for place, b in enumerate((1, 0) if j == 0 else (0, 1)):
             run_unit(j, b, place == 0)
@@ -380,6 +433,10 @@
         if j == 0:
             send_back(j, 0, pl.ds(0, 2))
         send_back(j, 1, pl.ds(0, 2))
+
+    for j in range(half):
+        for b in range(2):
+            local_slope(j, b)
 
     @pl.loop(0, 2 * half)
     def _(u):
@@ -400,8 +457,8 @@
 
     for j in range(half):
         for i in range(2):
-            key_terms(j, 0, i, slice(at3, at3 + height))
-            key_terms(j, 1, i, slice(at2, at3 + height))
+            for b in range(2):
+                key_terms(j, b, i, local_rows(b))
         sibling_copy(j).start()
 
     for j in range(half):
@@ -523,6 +580,7 @@
             pltpu.VMEM((half, 2, height, d), f32),
             pltpu.VMEM((2, 2, height, height), f32),
             pltpu.VMEM((height, height), bf16),
+            pltpu.VMEM((2, half, 1, group * height), f32),
             dma((2,)),
             dma((half,)), dma((half,)), dma((half,)), dma((half,)),
             dma((half, 2, 2)),
@@ -531,6 +589,7 @@
             dma((half, 2)),
             *[dma((half,))] * 3,
             dma, dma,
+            pltpu.SemaphoreType.REGULAR,
         ],
         compiler_params=pltpu.CompilerParams(
             collective_id=0, has_side_effects=True, vmem_limit_bytes=60 * 1024 * 1024

time: 26.2 us -> 25.6 us (0.977)
  Pallas kernels: 25.4 us -> 24.8 us
    pallas_call x1, Pallas kernels: 23.9 us -> 23.3 us  [per_device(): pl.pallas_call(functools.partial(kernel, n, kv_heads, group), out_shape=(...]
where the time goes in v6:
time: 25.6 us; the launch traced here: 25.5 us
  Pallas kernels  24.8 us (97%)
  between operations  0.64 us (2%)
    pallas_call x1, Pallas kernels, per_device(): pl.pallas_call(functools.partial(kernel, n, kv_heads, group), out_shape=(...  23.3 us
    pallas_call x1, Pallas kernels, per_device(): pl.pallas_call(functools.partial(write_out, kv_heads, span), out_shape=(j...  1.52 us

profile of v6, /device:TPU:0, one launch (start us, length us, event | category | flops | bytes accessed | tf_op | source)
XLA Modules:
  0.0 25.5 jit_solution(2257460233485921120)
XLA Ops:
  0.6 23.3 %shard_map.127 = (bf16[3,2,128,1024]{3,2,1,0:T(8,128)(2,1)S(1)}, bf16[3,2,128,1024]{3,2,1,0:T(8,128)(2,1)S(1)}, bf16[128,512]{1,0:T(8,128)(2,1)S(1)}, bf16[128,5...) custom-call(bf16[128,4096]{1,0:T(8,128)(2,1)} %q_hbm.1, bf16[128,4096]{1,0:T(8,128)(2,1)} %og_hbm.1, ...), custom_call_target="tpu_custom_call" | custom-call | tf_op jit(solution)/shard_map/pallas_call | solution.py:550
  23.9 1.5 %shard_map.128 = (bf16[128,4096]{1,0:T(8,128)(2,1)}, bf16[128,4096]{1,0:T(8,128)(2,1)}, bf16[128,512]{1,0:T(8,128)(2,1)}, bf16[128,512]{1,0:T(8,128)(2,1)}, f32[8,512]{1,0:T(8,128)}, /*index=5*/f32[8,512]{1,0:T(8,128)}) custom-call(bf16[3,2,128,1024]{3,2,1,0:T(8,128)(2,1)S(1)} %get-tuple-element.12.attn, bf16[3,2,128,1024]{3,2,1,0:T(8,128)(2,1)S(1)} %get-tuple-element.13.dq, ...), custom_call_target="tpu_custom_call" | custom-call | tf_op jit(solution)/shard_map/pallas_call | solution.py:601

commit v7 on v6

--- a/solution.py
+++ b/solution.py
@@ -26,7 +26,7 @@
     q_hbm, og_hbm, ak, av, pk, pv, w, lens,
     attn, dq, akg, avg, pkg, pvg,
     qog, kall, vt, kt, pgath, wst, lst, qs_t, cots, cots_t, p_all, ds_all, acc,
-    psend, precv, gsend, grecv, srecv, bias, tri_b, deltas,
+    psend, precv, gsend, grecv, srecv, bias, tri_b, deltas, early,
     small_sem, in_sem, kv_sem, xq_recv, xk_recv, win_recv, pg_recv, pr_recv, gr_recv, sr_recv, at_recv, dq_recv,
     xq_send, xk_send, win_send, pg_send, pr_send, gs_send, sr_send, at_send, dq_send, w_recv, w_send, go,
 ):
@@ -267,7 +267,7 @@
 
     for j in range(1, half):
         for i in range(2):
-            send_prompts(j, i)
+            send_window(j, i, core == 1)
     w_cross.wait_recv()
 
     @pl.loop(0, half)
@@ -275,21 +275,19 @@
         pltpu.make_async_copy(qog.at[0, j], qog.at[0, j], xq_recv.at[j]).wait()
         prepare(0, j)
 
+
     for j in range(1, half):
         for i in range(2):
-            send_window(j, i, True)
-    pltpu.make_async_copy(pgath.at[0, 0], pgath.at[0, 0], pg_recv.at[0, 0]).wait()
-
+            send_prompts(j, i)
+    for j in range(1, half):
+        for i in range(2):
+            send_window(j, i, core == 0)
     def assemble(j, i):
-        if j > 0 or i > 0:
-            pltpu.make_async_copy(pgath.at[j, i], pgath.at[j, i], pg_recv.at[j, i]).wait()
+        pltpu.make_async_copy(pgath.at[j, i], pgath.at[j, i], pg_recv.at[j, i]).wait()
         gathered = pgath[j, i].astype(jnp.float32).reshape(prompt, d)
         kall[j, i, :prompt, :] = gathered.astype(jnp.bfloat16)
 
     def arrive(j, i, b, leading):
-        if leading:
-            assemble(j, i)
-
         @pl.when(chip > 0)
         def _():
             for t in ((0,) if b == 0 else ()) + ((1,) if leading else ()):
@@ -307,31 +305,44 @@
         late = leading and j == 0
         if not late:
             arrive(j, 1, b, leading)
+            if leading:
+                assemble(j, 0)
+                assemble(j, 1)
 
         near_far = slice(prompt + b * height, prompt + (b + 3) * height)
         tri2 = twice(tri)
-        keys = jnp.concatenate([kall[j, 0, :prompt], kall[j, 0, near_far]], axis=0)
-
         def values():
             return jnp.concatenate([kall[j, 1, :prompt], kall[j, 1, near_far]], axis=0)
 
         if not late:
             vt[...] = values().T
         held = {}
+        tops = {}
 
         def rows_of(pair):
             return slice(pair * 2 * height, (pair + 1) * 2 * height)
 
+        def masked(scores):
+            far, near, own = scores[:height], scores[height : 2 * height], scores[2 * height :]
+            s_n = near + twice(bias[b, 0])
+            s_c = jnp.where(tri2, own, far) + twice(bias[b, 1])
+            return s_n, s_c, jnp.maximum(jnp.max(s_n, axis=0, keepdims=True), jnp.max(s_c, axis=0, keepdims=True))
+
+        def score_early(pair):
+            s_n, s_c, tops[pair] = masked(dot(kall[j, 0, near_far], qs_t[s, j, :, rows_of(pair)]))
+            early[pair, :height] = s_n
+            early[pair, height:] = s_c
+
         def score(pair):
-            scores = dot(keys, qs_t[s, j, :, rows_of(pair)])
-            s_p = scores[:at1]
-            s_n = scores[at2:at3] + twice(bias[b, 0])
-            s_c = jnp.where(tri2, scores[at3:], scores[at1:at2]) + twice(bias[b, 1])
-            top = jnp.maximum(
-                jnp.maximum(jnp.max(s_p, axis=0, keepdims=True), jnp.max(s_n, axis=0, keepdims=True)),
-                jnp.max(s_c, axis=0, keepdims=True),
-            )
-            held[pair] = s_p, s_n, s_c, top
+            if late:
+                s_p = dot(kall[j, 0, :prompt], qs_t[s, j, :, rows_of(pair)])
+                s_n, s_c, top = early[pair, :height], early[pair, height:], tops[pair]
+            else:
+                keys = jnp.concatenate([kall[j, 0, :prompt], kall[j, 0, near_far]], axis=0)
+                scores = dot(keys, qs_t[s, j, :, rows_of(pair)])
+                s_p = scores[:at1]
+                s_n, s_c, top = masked(scores[at1:])
+            held[pair] = s_p, s_n, s_c, jnp.maximum(top, jnp.max(s_p, axis=0, keepdims=True))
 
         def soften(pair):
             rows = rows_of(pair)
@@ -378,13 +389,18 @@
             ds_all[s, j, rows, lanes] = p_all[s, j, rows, lanes] * (slopes - delta).astype(jnp.bfloat16)
 
         pairs = group // 2
+        if late:
+            for pair in range(pairs):
+                score_early(pair)
+            assemble(j, 0)
         for step in range(-2, pairs + 2):
             if 0 <= step < pairs:
                 soften(step)
             if 0 <= step + 2 < pairs:
                 score(step + 2)
-            if late and step == 0:
+            if late and step == 1:
                 arrive(j, 1, b, leading)
+                assemble(j, 1)
                 vt[...] = values().T
             if 0 <= step - 1 < pairs:
                 attend(step - 1)
@@ -425,12 +441,10 @@
             ).astype(jnp.bfloat16)
 
     for j in range(half):
-        for place, b in enumerate((1, 0) if j == 0 else (0, 1)):
+        for place, b in enumerate((1, 0)):
             run_unit(j, b, place == 0)
-            if j > 0 and b == 0:
-                send_back(j, 0, pl.ds(0, 2))
         send_reduce(j, pl.ds(0, 2))
-        if j == 0:
+        if True:
             send_back(j, 0, pl.ds(0, 2))
         send_back(j, 1, pl.ds(0, 2))
 
@@ -581,6 +595,7 @@
             pltpu.VMEM((2, 2, height, height), f32),
             pltpu.VMEM((height, height), bf16),
             pltpu.VMEM((2, half, 1, group * height), f32),
+            pltpu.VMEM((group // 2, 2 * height, 2 * height), f32),
             dma((2,)),
             dma((half,)), dma((half,)), dma((half,)), dma((half,)),
             dma((half, 2, 2)),

time: 25.6 us -> 25.1 us (0.980); the launches traced: 25.5 us -> 24.6 us
  Pallas kernels: 24.8 us -> 24 us
    pallas_call x1, Pallas kernels: 23.3 us -> 22.5 us  [per_device(): pl.pallas_call(functools.partial(kernel, n, kv_heads, group), out_shape=(...]
where the time goes in v7:
time: 25.1 us; the launch traced here: 24.6 us
  Pallas kernels  24 us (96%)
  between operations  0.64 us (3%)
    pallas_call x1, Pallas kernels, per_device(): pl.pallas_call(functools.partial(kernel, n, kv_heads, group), out_shape=(...  22.5 us
    pallas_call x1, Pallas kernels, per_device(): pl.pallas_call(functools.partial(write_out, kv_heads, span), out_shape=(j...  1.52 us

profile of v7, /device:TPU:0, one launch (start us, length us, event | category | flops | bytes accessed | tf_op | source)
XLA Modules:
  0.0 24.6 jit_solution(4595789392703559383)
XLA Ops:
  0.6 22.5 %shard_map.127 = (bf16[3,2,128,1024]{3,2,1,0:T(8,128)(2,1)S(1)}, bf16[3,2,128,1024]{3,2,1,0:T(8,128)(2,1)S(1)}, bf16[128,512]{1,0:T(8,128)(2,1)S(1)}, bf16[128,5...) custom-call(bf16[128,4096]{1,0:T(8,128)(2,1)} %q_hbm.1, bf16[128,4096]{1,0:T(8,128)(2,1)} %og_hbm.1, ...), custom_call_target="tpu_custom_call" | custom-call | tf_op jit(solution)/shard_map/pallas_call | solution.py:564
  23.1 1.5 %shard_map.128 = (bf16[128,4096]{1,0:T(8,128)(2,1)}, bf16[128,4096]{1,0:T(8,128)(2,1)}, bf16[128,512]{1,0:T(8,128)(2,1)}, bf16[128,512]{1,0:T(8,128)(2,1)}, f32[8,512]{1,0:T(8,128)}, /*index=5*/f32[8,512]{1,0:T(8,128)}) custom-call(bf16[3,2,128,1024]{3,2,1,0:T(8,128)(2,1)S(1)} %get-tuple-element.12.attn, bf16[3,2,128,1024]{3,2,1,0:T(8,128)(2,1)S(1)} %get-tuple-element.13.dq, ...), custom_call_target="tpu_custom_call" | custom-call | tf_op jit(solution)/shard_map/pallas_call | solution.py:616

commit v8 on v7

--- a/solution.py
+++ b/solution.py
@@ -221,6 +221,9 @@
         send_prompts(0, i)
     send_window(0, 1, core == 0)
 
+    for j in range(1, half):
+        for i in range(2):
+            send_window(j, i, core == 1)
     acc[...] = jnp.zeros(acc.shape, jnp.float32)
 
     @pl.when(chip == 0)
@@ -265,9 +268,6 @@
         pltpu.make_async_copy(qog.at[1, j], qog.at[1, j], in_sem.at[j]).wait()
         prepare(1, j)
 
-    for j in range(1, half):
-        for i in range(2):
-            send_window(j, i, core == 1)
     w_cross.wait_recv()
 
     @pl.loop(0, half)

time: 25.1 us -> 24.9 us (level)
  no operation moved by 1% of the time
where the time goes in v8:
time: 24.9 us; the launch traced here: 24.6 us
  Pallas kernels  24 us (96%)
  between operations  0.64 us (3%)
    pallas_call x1, Pallas kernels, per_device(): pl.pallas_call(functools.partial(kernel, n, kv_heads, group), out_shape=(...  22.5 us
    pallas_call x1, Pallas kernels, per_device(): pl.pallas_call(functools.partial(write_out, kv_heads, span), out_shape=(j...  1.52 us

profile of v8, /device:TPU:0, one launch (start us, length us, event | category | flops | bytes accessed | tf_op | source)
XLA Modules:
  0.0 24.6 jit_solution(9557358706402372535)
XLA Ops:
  0.6 22.5 %shard_map.127 = (bf16[3,2,128,1024]{3,2,1,0:T(8,128)(2,1)S(1)}, bf16[3,2,128,1024]{3,2,1,0:T(8,128)(2,1)S(1)}, bf16[128,512]{1,0:T(8,128)(2,1)S(1)}, bf16[128,5...) custom-call(bf16[128,4096]{1,0:T(8,128)(2,1)} %q_hbm.1, bf16[128,4096]{1,0:T(8,128)(2,1)} %og_hbm.1, ...), custom_call_target="tpu_custom_call" | custom-call | tf_op jit(solution)/shard_map/pallas_call | solution.py:564
  23.1 1.5 %shard_map.128 = (bf16[128,4096]{1,0:T(8,128)(2,1)}, bf16[128,4096]{1,0:T(8,128)(2,1)}, bf16[128,512]{1,0:T(8,128)(2,1)}, bf16[128,512]{1,0:T(8,128)(2,1)}, f32[8,512]{1,0:T(8,128)}, /*index=5*/f32[8,512]{1,0:T(8,128)}) custom-call(bf16[3,2,128,1024]{3,2,1,0:T(8,128)(2,1)S(1)} %get-tuple-element.12.attn, bf16[3,2,128,1024]{3,2,1,0:T(8,128)(2,1)S(1)} %get-tuple-element.13.dq, ...), custom_call_target="tpu_custom_call" | custom-call | tf_op jit(solution)/shard_map/pallas_call | solution.py:616
